TPU v7x, 32 devices: a whole 2x2x4 slice. The times are simulated.
32 devices in a mesh: context: 4 (over z), fsdp: 4 (over x, core), heads: 2 (over y).
Axes of the slice: x: 2, y: 2, z: 4, core: 2. Of those that a mesh axis runs over, the one named last changes fastest.
Arguments:
- layer_input: bfloat16 [2048, 2048], P(('context', 'fsdp')), may hold values from -6 to 6
- block_pair: int32 [4], replicated, may hold values from 0 to 3, each once
- attn_gain: bfloat16 [2048], P(('context', 'fsdp')), may hold values from 0.099609375 to 1.8984375
- q_weight: bfloat16 [2048, 2048], P(('context', 'fsdp'), 'heads'), may hold values from -0.125 to 0.125
- key_projection: bfloat16 [2048, 1024], P(('context', 'fsdp'), 'heads'), may hold values from -0.125 to 0.125
- value_projection: bfloat16 [2048, 1024], P(('context', 'fsdp'), 'heads'), may hold values from -0.125 to 0.125
- q_gain: bfloat16 [128], P(('context', 'fsdp')), may hold values from 0.8 to 5
- k_gain: bfloat16 [128], P(('context', 'fsdp')), may hold values from 0.8 to 5
- o_weight: bfloat16 [2048, 2048], P('heads', ('context', 'fsdp')), may hold values from -0.75 to 0.75
- mlp_gain: bfloat16 [2048], P(('context', 'fsdp')), may hold values from 0.099609375 to 1.8984375
- gate_weight: bfloat16 [2048, 6144], P(('context', 'fsdp'), 'heads'), may hold values from -0.125 to 0.125
- up_weight: bfloat16 [2048, 6144], P(('context', 'fsdp'), 'heads'), may hold values from -0.125 to 0.125
- down_weight: bfloat16 [6144, 2048], P('heads', ('context', 'fsdp')), may hold values from -0.078125 to 0.078125
- cotangent: bfloat16 [2048, 2048], P(('context', 'fsdp')), may hold values from -6 to 6
Outputs:
- block_out: bfloat16 [2048, 2048], P(('context', 'fsdp'))
- input_grad: float32 [2048, 2048], P(('context', 'fsdp'))
- attn_gain_grad: float32 [2048], P(('context', 'fsdp'))
- q_weight_grad: float32 [2048, 2048], P(('context', 'fsdp'), 'heads')
- k_weight_grad: float32 [2048, 1024], P(('context', 'fsdp'), 'heads')
- v_weight_grad: float32 [2048, 1024], P(('context', 'fsdp'), 'heads')
- q_gain_grad: float32 [128], P(('context', 'fsdp'))
- k_gain_grad: float32 [128], P(('context', 'fsdp'))
- o_weight_grad: float32 [2048, 2048], P('heads', ('context', 'fsdp'))
- mlp_gain_grad: float32 [2048], P(('context', 'fsdp'))
- gate_weight_grad: float32 [2048, 6144], P(('context', 'fsdp'), 'heads')
- up_weight_grad: float32 [2048, 6144], P(('context', 'fsdp'), 'heads')
- down_weight_grad: float32 [6144, 2048], P('heads', ('context', 'fsdp'))
Inputs may be any that keep to these rules, and one draw needn't show every extreme that they name: `block_pair`: each of 0 to 3 appears once.
All inputs are finite; a program needn't handle non-finite values.
Results may differ from a plain program's by a relative error of at most 0.025.
The roundings to bfloat16 on the way count: a program that leaves them out, or rounds other values in their place, can miss the bound.
Values may be sent and summed in bfloat16 or wider, within the bound.
A program may use at most 256 MiB of HBM per device.

v0:
```python
import functools
import math

import jax
import jax.numpy as jnp
from jax import lax
from jax.experimental import pallas as pl
from jax.experimental.pallas import tpu as pltpu
from jax.sharding import PartitionSpec as P

HEAD_SIZE = 128
CONTEXT, FSDP, HEADS = "context", "fsdp", "heads"
ROWS = (CONTEXT, FSDP)


EPS = 1e-06
THETA = 1000000.0
NEG = -1e30


def row_places(block_pair, row_ids, block_len):
    owners = block_pair.shape[0]
    holder = row_ids // (2 * block_len)
    within = row_ids % (2 * block_len)
    match = holder[:, None] == jnp.arange(owners, dtype=jnp.int32)[None, :]
    paired = jnp.sum(jnp.where(match, block_pair[None, :], 0), axis=1)
    which = jnp.where(within >= block_len, 2 * owners - 1 - paired, paired)
    return which * block_len + within % block_len


def rope_tables(places, head_dim):
    half = head_dim // 2
    freq = jnp.exp(jnp.arange(half, dtype=jnp.float32) * (-2.0 * math.log(THETA) / head_dim))
    angle = places.astype(jnp.float32)[:, None] * freq[None, :]
    return (jnp.cos(angle)[:, None, :], jnp.sin(angle)[:, None, :])


def apply_rotary(field, cosine_table, sine_table):
    half = field.shape[-1] // 2
    first = field[..., :half]
    second = field[..., half:]
    return jnp.concatenate(
        [first * cosine_table - second * sine_table, second * cosine_table + first * sine_table],
        axis=-1,
    )


def unrotate(grad, cosine_table, sine_table):
    half = grad.shape[-1] // 2
    first = grad[..., :half]
    second = grad[..., half:]
    return jnp.concatenate(
        [first * cosine_table + second * sine_table, second * cosine_table - first * sine_table],
        axis=-1,
    )


def row_norm(field):
    factor = lax.rsqrt(jnp.mean(field * field, axis=-1, keepdims=True) + EPS)
    return (field * factor, factor)


def norm_backward(grad_hat, normed, factor):
    return factor * (grad_hat - normed * jnp.mean(grad_hat * normed, axis=-1, keepdims=True))


def masked_scores(query_matrix, key_rows, query_places, key_places, softmax_scale):
    score_matrix = (
        jnp.einsum("oblh,wbh->blow", query_matrix, key_rows, preferred_element_type=jnp.float32)
        * softmax_scale
    )
    allowed = key_places[None, :] <= query_places[:, None]
    return (jnp.where(allowed, score_matrix, NEG), allowed)


def per_device(
    layer_input,
    block_pair,
    attn_gain,
    q_weight,
    key_projection,
    value_projection,
    q_gain,
    k_gain,
    o_weight,
    mlp_gain,
    gate_weight,
    up_weight,
    down_weight,
    cotangent,
):
    wide_float_type = jnp.float32
    narrow_float_type = jnp.bfloat16
    tokens = layer_input.shape[0]
    members = lax.axis_size(ROWS)
    seq_len = tokens * members
    block_len = tokens * lax.axis_size(FSDP) // 2
    kv_local = key_projection.shape[1] // HEAD_SIZE
    q_local = q_weight.shape[1] // HEAD_SIZE
    group_size = q_local // kv_local
    softmax_scale = 1.0 / math.sqrt(HEAD_SIZE)
    (
        full_attn_gain,
        full_q,
        full_k,
        full_v,
        full_q_gain,
        full_k_gain,
        full_o,
        full_mlp_gain,
        full_gate,
        full_up,
        full_down,
    ) = (
        lax.all_gather(attn_gain, ROWS, axis=0, tiled=True),
        lax.all_gather(q_weight, ROWS, axis=0, tiled=True),
        lax.all_gather(key_projection, ROWS, axis=0, tiled=True),
        lax.all_gather(value_projection, ROWS, axis=0, tiled=True),
        lax.all_gather(q_gain, ROWS, axis=0, tiled=True),
        lax.all_gather(k_gain, ROWS, axis=0, tiled=True),
        lax.all_gather(o_weight, ROWS, axis=1, tiled=True),
        lax.all_gather(mlp_gain, ROWS, axis=0, tiled=True),
        lax.all_gather(gate_weight, ROWS, axis=0, tiled=True),
        lax.all_gather(up_weight, ROWS, axis=0, tiled=True),
        lax.all_gather(down_weight, ROWS, axis=1, tiled=True),
    )
    own_rows = lax.axis_index(ROWS) * tokens + jnp.arange(tokens, dtype=jnp.int32)
    own_places = row_places(block_pair, own_rows, block_len)
    cosine_table, sine_table = rope_tables(own_places, HEAD_SIZE)
    x_full = layer_input.astype(wide_float_type)
    x_hat, x_scale = row_norm(x_full)
    attn_scale = full_attn_gain.astype(wide_float_type)
    normalized_input = (x_hat * attn_scale).astype(narrow_float_type)
    q_raw = jnp.dot(normalized_input, full_q, preferred_element_type=wide_float_type).reshape(
        tokens, q_local, HEAD_SIZE
    )
    unnormalized_keys = jnp.dot(
        normalized_input, full_k, preferred_element_type=wide_float_type
    ).reshape(tokens, kv_local, HEAD_SIZE)
    value_rows_backward = jnp.dot(
        normalized_input, full_v, preferred_element_type=wide_float_type
    ).astype(narrow_float_type)
    normalized_queries, q_scale = row_norm(q_raw)
    normalized_keys, key_norm_scale = row_norm(unnormalized_keys)
    query_gain_vector = full_q_gain.astype(wide_float_type)
    key_gain_vector = full_k_gain.astype(wide_float_type)
    rotated_queries = apply_rotary(
        normalized_queries * query_gain_vector, cosine_table, sine_table
    ).astype(narrow_float_type)
    grouped_queries = rotated_queries.reshape(tokens, kv_local, group_size, HEAD_SIZE)
    k_flat = (
        apply_rotary(normalized_keys * key_gain_vector, cosine_table, sine_table)
        .astype(narrow_float_type)
        .reshape(tokens, kv_local * HEAD_SIZE)
    )
    start_state = (
        jnp.full((kv_local, group_size, tokens), NEG, wide_float_type),
        jnp.zeros((kv_local, group_size, tokens), wide_float_type),
        jnp.zeros((kv_local, group_size, tokens, HEAD_SIZE), wide_float_type),
    )
    key_piece = lax.all_gather(k_flat, ROWS, axis=0, tiled=True)
    value_piece = lax.all_gather(value_rows_backward, ROWS, axis=0, tiled=True)
    count = key_piece.shape[0]
    width = math.gcd(count, 512)
    steps_here = count // width
    key_blocks = key_piece.reshape(steps_here, width, kv_local, HEAD_SIZE)
    value_blocks = value_piece.reshape(steps_here, width, kv_local, HEAD_SIZE)
    key_places = row_places(block_pair, jnp.arange(count, dtype=jnp.int32), block_len).reshape(
        steps_here, width
    )

    def online(state, blockset):
        top, total, softmax_numerator = state
        key_tile, value_tile, place_blk = blockset
        score_matrix, allowed = masked_scores(
            grouped_queries, key_tile, own_places, place_blk, softmax_scale
        )
        new_top = jnp.maximum(top, jnp.max(score_matrix, axis=-1))
        shrink = jnp.exp(top - new_top)
        weight_set = jnp.where(allowed, jnp.exp(score_matrix - new_top[..., None]), 0.0)
        total = total * shrink + jnp.sum(weight_set, axis=-1)
        softmax_numerator = softmax_numerator * shrink[..., None] + jnp.einsum(
            "nwqf,fny->nwqy",
            weight_set.astype(narrow_float_type),
            value_tile,
            preferred_element_type=wide_float_type,
        )
        return ((new_top, total, softmax_numerator), None)

    result, _ = lax.scan(online, start_state, (key_blocks, value_blocks, key_places))
    top, total, softmax_numerator = result
    log_total = top + jnp.log(total)
    attention_backward = (
        jnp.transpose(softmax_numerator / total[..., None], (2, 0, 1, 3))
        .reshape(tokens, q_local * HEAD_SIZE)
        .astype(narrow_float_type)
    )
    attn_part = jnp.dot(attention_backward, full_o, preferred_element_type=wide_float_type)
    hidden = x_full + lax.psum(attn_part, HEADS)
    mlp_scale = full_mlp_gain.astype(wide_float_type)
    h_hat, h_scale = row_norm(hidden)
    h_normed = (h_hat * mlp_scale).astype(narrow_float_type)
    gate = jnp.dot(h_normed, full_gate, preferred_element_type=wide_float_type)
    up_val = jnp.dot(h_normed, full_up, preferred_element_type=wide_float_type)
    sigma = jax.nn.sigmoid(gate)
    silu = gate * sigma
    act = (silu * up_val).astype(narrow_float_type)
    mlp_part = jnp.dot(act, full_down, preferred_element_type=wide_float_type)
    block_out = (hidden + lax.psum(mlp_part, HEADS)).astype(narrow_float_type)
    (
        full_attn_gain,
        full_q,
        full_k,
        full_v,
        full_q_gain,
        full_k_gain,
        full_o,
        full_mlp_gain,
        full_gate,
        full_up,
        full_down,
    ) = (
        lax.all_gather(attn_gain, ROWS, axis=0, tiled=True),
        lax.all_gather(q_weight, ROWS, axis=0, tiled=True),
        lax.all_gather(key_projection, ROWS, axis=0, tiled=True),
        lax.all_gather(value_projection, ROWS, axis=0, tiled=True),
        lax.all_gather(q_gain, ROWS, axis=0, tiled=True),
        lax.all_gather(k_gain, ROWS, axis=0, tiled=True),
        lax.all_gather(o_weight, ROWS, axis=1, tiled=True),
        lax.all_gather(mlp_gain, ROWS, axis=0, tiled=True),
        lax.all_gather(gate_weight, ROWS, axis=0, tiled=True),
        lax.all_gather(up_weight, ROWS, axis=0, tiled=True),
        lax.all_gather(down_weight, ROWS, axis=1, tiled=True),
    )
    grad_downw = jnp.einsum("tf,td->fd", act, cotangent, preferred_element_type=wide_float_type)
    grad_act = jnp.einsum("td,fd->tf", cotangent, full_down, preferred_element_type=wide_float_type)
    grad_g = (grad_act * up_val * (sigma * (1.0 + gate * (1.0 - sigma)))).astype(narrow_float_type)
    grad_u = (grad_act * silu).astype(narrow_float_type)
    grad_gatew = jnp.einsum("tc,tf->cf", h_normed, grad_g, preferred_element_type=wide_float_type)
    grad_upw = jnp.einsum("tc,tf->cf", h_normed, grad_u, preferred_element_type=wide_float_type)
    normed_part = jnp.einsum(
        "tf,cf->tc", grad_g, full_gate, preferred_element_type=wide_float_type
    ) + jnp.einsum("tf,cf->tc", grad_u, full_up, preferred_element_type=wide_float_type)
    grad_normed = lax.psum(normed_part, HEADS)
    grad_mlp_gain = jnp.sum(grad_normed * h_hat, axis=0)
    grad_h = cotangent.astype(wide_float_type) + norm_backward(
        grad_normed * mlp_scale, h_hat, h_scale
    )
    grad_hb = grad_h.astype(narrow_float_type)
    grad_ow = jnp.einsum(
        "tq,td->qd", attention_backward, grad_hb, preferred_element_type=wide_float_type
    )
    output_gradient_backward = jnp.einsum(
        "td,qd->tq", grad_hb, full_o, preferred_element_type=wide_float_type
    ).astype(narrow_float_type)
    grouped_output_gradient = output_gradient_backward.reshape(
        tokens, kv_local, group_size, HEAD_SIZE
    )
    delta_rows = jnp.sum(
        grouped_output_gradient.astype(wide_float_type)
        * attention_backward.reshape(tokens, kv_local, group_size, HEAD_SIZE).astype(
            wide_float_type
        ),
        axis=-1,
    )
    delta_rows = jnp.transpose(delta_rows, (1, 2, 0))
    keys_all, values_all = (
        lax.all_gather(k_flat, ROWS, axis=0, tiled=True),
        lax.all_gather(value_rows_backward, ROWS, axis=0, tiled=True),
    )
    width = math.gcd(seq_len, 512)
    steps_all = seq_len // width
    all_places = row_places(block_pair, jnp.arange(seq_len, dtype=jnp.int32), block_len).reshape(
        steps_all, width
    )

    def backward_step(grad_q_acc, blockset):
        key_tile, value_tile, place_blk = blockset
        score_matrix, allowed = masked_scores(
            grouped_queries, key_tile, own_places, place_blk, softmax_scale
        )
        probability_rows = jnp.where(allowed, jnp.exp(score_matrix - log_total[..., None]), 0.0)
        grad_v_blk = jnp.einsum(
            "mojp,jmof->pmf",
            probability_rows.astype(narrow_float_type),
            grouped_output_gradient,
            preferred_element_type=wide_float_type,
        )
        probability_gradient = jnp.einsum(
            "oblh,wbh->blow",
            grouped_output_gradient,
            value_tile,
            preferred_element_type=wide_float_type,
        )
        score_gradient = (probability_rows * (probability_gradient - delta_rows[..., None])).astype(
            narrow_float_type
        )
        grad_q_acc = (
            grad_q_acc
            + jnp.einsum(
                "xwzq,qxp->zxwp", score_gradient, key_tile, preferred_element_type=wide_float_type
            )
            * softmax_scale
        )
        grad_k_blk = (
            jnp.einsum(
                "mojp,jmof->pmf",
                score_gradient,
                grouped_queries,
                preferred_element_type=wide_float_type,
            )
            * softmax_scale
        )
        return (grad_q_acc, (grad_k_blk, grad_v_blk))

    rotated_query_gradient, stacked = lax.scan(
        backward_step,
        jnp.zeros((tokens, kv_local, group_size, HEAD_SIZE), wide_float_type),
        (
            keys_all.reshape(steps_all, width, kv_local, HEAD_SIZE),
            values_all.reshape(steps_all, width, kv_local, HEAD_SIZE),
            all_places,
        ),
    )
    grad_k_all = stacked[0].reshape(seq_len, kv_local * HEAD_SIZE)
    grad_v_all = stacked[1].reshape(seq_len, kv_local * HEAD_SIZE)
    grad_k_own, grad_v_own = (
        lax.psum_scatter(grad_k_all, ROWS, scatter_dimension=0, tiled=True),
        lax.psum_scatter(grad_v_all, ROWS, scatter_dimension=0, tiled=True),
    )
    grad_qg = unrotate(
        rotated_query_gradient.reshape(tokens, q_local, HEAD_SIZE), cosine_table, sine_table
    )
    q_gain_part = jnp.sum(grad_qg * normalized_queries, axis=(0, 1))
    query_gradient = (
        norm_backward(grad_qg * query_gain_vector, normalized_queries, q_scale)
        .reshape(tokens, q_local * HEAD_SIZE)
        .astype(narrow_float_type)
    )
    key_gain_gradient = unrotate(
        grad_k_own.reshape(tokens, kv_local, HEAD_SIZE), cosine_table, sine_table
    )
    k_gain_part = jnp.sum(key_gain_gradient * normalized_keys, axis=(0, 1))
    key_gradient = (
        norm_backward(key_gain_gradient * key_gain_vector, normalized_keys, key_norm_scale)
        .reshape(tokens, kv_local * HEAD_SIZE)
        .astype(narrow_float_type)
    )
    value_gradient_backward = grad_v_own.astype(narrow_float_type)
    grad_qw = jnp.einsum(
        "tc,tq->cq", normalized_input, query_gradient, preferred_element_type=wide_float_type
    )
    grad_kw = jnp.einsum(
        "tc,tq->cq", normalized_input, key_gradient, preferred_element_type=wide_float_type
    )
    grad_vw = jnp.einsum(
        "tc,tq->cq",
        normalized_input,
        value_gradient_backward,
        preferred_element_type=wide_float_type,
    )
    xn_part = (
        jnp.einsum("tq,cq->tc", query_gradient, full_q, preferred_element_type=wide_float_type)
        + jnp.einsum("tq,cq->tc", key_gradient, full_k, preferred_element_type=wide_float_type)
        + jnp.einsum(
            "tq,cq->tc", value_gradient_backward, full_v, preferred_element_type=wide_float_type
        )
    )
    grad_xn, grad_q_gain, grad_k_gain = lax.psum((xn_part, q_gain_part, k_gain_part), HEADS)
    grad_attn_gain = jnp.sum(grad_xn * x_hat, axis=0)
    input_grad = grad_h + norm_backward(grad_xn * attn_scale, x_hat, x_scale)
    owned = (
        lax.psum_scatter(grad_attn_gain, ROWS, scatter_dimension=0, tiled=True),
        lax.psum_scatter(grad_qw, ROWS, scatter_dimension=0, tiled=True),
        lax.psum_scatter(grad_kw, ROWS, scatter_dimension=0, tiled=True),
        lax.psum_scatter(grad_vw, ROWS, scatter_dimension=0, tiled=True),
        lax.psum_scatter(grad_q_gain, ROWS, scatter_dimension=0, tiled=True),
        lax.psum_scatter(grad_k_gain, ROWS, scatter_dimension=0, tiled=True),
        lax.psum_scatter(grad_ow, ROWS, scatter_dimension=1, tiled=True),
        lax.psum_scatter(grad_mlp_gain, ROWS, scatter_dimension=0, tiled=True),
        lax.psum_scatter(grad_gatew, ROWS, scatter_dimension=0, tiled=True),
        lax.psum_scatter(grad_upw, ROWS, scatter_dimension=0, tiled=True),
        lax.psum_scatter(grad_downw, ROWS, scatter_dimension=1, tiled=True),
    )
    return (
        block_out,
        input_grad,
        owned[0],
        owned[1],
        owned[2],
        owned[3],
        owned[4],
        owned[5],
        owned[6],
        owned[7],
        owned[8],
        owned[9],
        owned[10],
    )


MESH = pl.DeviceIdType.MESH
HBM = pl.BlockSpec(memory_space=pltpu.HBM)
VM = pl.BlockSpec(memory_space=pltpu.VMEM)
SLOTS = 160
NT = (((1,), (1,)), ((), ()))
TN = (((0,), (0,)), ((), ()))
BF = jnp.bfloat16
F32 = jnp.float32


class Net:
    def __init__(self, shards, send, recv, loc):
        self.C = shards
        self.send, self.recv, self.loc = send, recv, loc
        self.used = self.used_local = 0
        self.c, f, self.y = (lax.axis_index(a) for a in (CONTEXT, FSDP, HEADS))
        self.x, self.k = f // 2, f % 2

    def at(self, c=None, x=None, k=None, y=None):
        c, x, k, y = (own if v is None else v for v, own in ((c, self.c), (x, self.x), (k, self.k), (y, self.y)))
        return (c, 2 * x + k, y)

    def core(self):
        return self.at(k=1 - self.k)

    def over_x(self):
        return self.at(x=1 - self.x)

    def over_y(self):
        return self.at(y=1 - self.y)

    def shard(self, step):
        return lax.rem(self.c + step + self.C, self.C)

    def slot(self):
        self.used += 1
        return self.used - 1

    def remote(self, src, dst, slot, to):
        return pltpu.make_async_remote_copy(
            src_ref=src, dst_ref=dst, send_sem=self.send.at[slot], recv_sem=self.recv.at[slot],
            device_id=to, device_id_type=MESH,
        )

    def local(self, src, dst):
        self.used_local += 1
        return pltpu.make_async_copy(src, dst, self.loc.at[self.used_local - 1])

    def meet(self, devices):
        barrier = pltpu.get_barrier_semaphore()
        for to in devices:
            pl.semaphore_signal(barrier, inc=1, device_id=to, device_id_type=MESH)
        pl.semaphore_wait(barrier, len(devices))

    def group(self):
        return [
            self.at(c=self.shard(dc), k=(self.k + dk) % 2)
            for dc in range(self.C) for dk in range(2) if (dc, dk) != (0, 0)
        ]


def run(*parts):
    live = list(parts)
    while live:
        live = [p for p in live if next(p, 0) != 0]


def gather_rows(net, src, dst, half):
    C, c, k, y = net.C, net.c, net.k, net.y
    H = dst.shape[-1] // 2
    mine = pl.ds(pl.multiple_of(y * H, 128), H)
    other = pl.ds(pl.multiple_of((1 - y) * H, 128), H)
    own_cols = mine if half else pl.ds(0, 2 * H)
    own_half = src if half else src.at[:, mine]
    right, left = net.at(c=c + 1), net.at(c=c - 1)
    core, over_y = net.core(), net.over_y()
    keep = net.local(src, dst.at[k, c, :, own_cols])
    keep.start()
    hops = [(d, s) for s in range(1, C) for d in (0, 1)]
    zslot = {h: net.slot() for h in hops}
    yslot = {h: net.slot() for h in hops}
    aslot = {h: net.slot() for h in hops}
    bslot = {h: net.slot() for h in hops}
    own_core, own_y, own_core2 = net.slot(), net.slot(), net.slot()
    no_right, no_left = c < C - 1, c > 0

    def chunk(d, s):
        return (c - s, c - s >= 0) if d == 0 else (c + s, c + s < C)

    def z_send(d, s, source, q):
        to = right if d == 0 else left
        return net.remote(source, dst.at[k, q, :, mine], zslot[d, s], to)

    @pl.when(no_right)
    def _():
        z_send(0, 1, own_half, c).start()

    @pl.when(no_left)
    def _():
        z_send(1, 1, own_half, c).start()

    to_core = net.remote(src, dst.at[k, c, :, own_cols], own_core, core)
    to_core.start()
    if half:
        to_y = net.remote(src, dst.at[k, c, :, mine], own_y, over_y)
        to_y.start()
    yield 1
    for d, s in hops:
        q, valid = chunk(d, s)

        @pl.when(valid)
        def _(d=d, s=s, q=q):
            piece = dst.at[k, q, :, mine]
            z_send(d, s, piece, q).wait_recv()
            if s < C - 1:
                @pl.when(no_right if d == 0 else no_left)
                def _():
                    z_send(d, s + 1, piece, q).start()
            net.remote(piece, piece, yslot[d, s], over_y).start()
            net.remote(piece, piece, aslot[d, s], core).start()
        yield 1
    if half:
        piece = dst.at[k, c, :, other]
        net.remote(piece, piece, own_y, over_y).wait_recv()
        net.remote(piece, piece, own_core2, core).start()
    for d, s in hops:
        q, valid = chunk(d, s)

        @pl.when(valid)
        def _(d=d, s=s, q=q):
            piece = dst.at[k, q, :, other]
            net.remote(piece, piece, yslot[d, s], over_y).wait_recv()
            net.remote(piece, piece, bslot[d, s], core).start()
        yield 1
    to_core_in = net.remote(src, dst.at[1 - k, c, :, own_cols], own_core, core)
    to_core_in.wait_recv()
    to_core_in.wait_send()
    if half:
        piece = dst.at[1 - k, c, :, other]
        net.remote(piece, piece, own_core2, core).wait()
        to_y.wait_send()
    for d, s in hops:
        q, valid = chunk(d, s)

        @pl.when(valid)
        def _(d=d, s=s, q=q):
            a, b = dst.at[1 - k, q, :, mine], dst.at[1 - k, q, :, other]
            net.remote(a, a, aslot[d, s], core).wait()
            net.remote(b, b, bslot[d, s], core).wait()
            net.remote(a, a, yslot[d, s], over_y).wait_send()

        sent = jnp.logical_and(no_right if d == 0 else no_left, chunk(d, s - 1)[1])

        @pl.when(sent)
        def _(d=d, s=s):
            piece = dst.at[k, c, :, mine]
            z_send(d, s, piece, c).wait_send()
    keep.wait()
    yield 1


def deal_weights(net, groups):
    C, c, x, k = net.C, net.c, net.x, net.k
    steps = [(dc, dk) for dc in range(C) for dk in range(2)]
    zs = {(g, s): net.slot() for s in steps for g in range(len(groups))}
    xs = {(g, s): net.slot() for s in steps for g in range(len(groups))}
    mine = c * 4 + 2 * x + k
    keeps = []
    for s in steps[1:] + steps[:1]:
        dc, dk = s
        tc, tk = net.shard(dc), (k + dk) % 2
        for g, (pieces, whole) in enumerate(groups):
            for src, pick, put in pieces:
                if s == (0, 0):
                    net.remote(src.at[pick(tc, tk)], put(mine), xs[g, s], net.over_x()).start()
                    keep = net.local(src.at[pick(tc, tk)], put(mine))
                    keep.start()
                    keeps.append(keep)
                else:
                    net.remote(src.at[pick(tc, tk)], put(mine), zs[g, s], net.at(c=tc, k=tk)).start()
        if dk:
            yield 1
    for s in steps[1:]:
        dc, dk = s
        fc, fk = net.shard(-dc), (k + dk) % 2
        for g, (pieces, whole) in enumerate(groups):
            block = whole(fc * 4 + 2 * x + fk)
            net.remote(block, block, zs[g, s], net.over_x()).wait_recv()
            net.remote(block, block, xs[g, s], net.over_x()).start()
        yield 1
    for s in steps:
        dc, dk = s
        fc, fk = net.shard(-dc), (k + dk) % 2
        for g, (pieces, whole) in enumerate(groups):
            block = whole(fc * 4 + 2 * (1 - x) + fk)
            net.remote(block, block, xs[g, s], net.over_x()).wait()
            if s != (0, 0):
                net.remote(block, block, zs[g, s], net.over_x()).wait_send()
        yield 1
    for keep in keeps:
        keep.wait()
    yield 1


def reduce_scratch(C, rows, width, tiles):
    w = width // tiles
    return [
        pltpu.VMEM((tiles, C, rows, w), BF),
        pltpu.VMEM((tiles, C, rows, w), BF),
        pltpu.VMEM((tiles // 2, C, rows, w), BF),
        pltpu.VMEM((tiles // 2, C, rows, w), BF),
        pltpu.VMEM((tiles // 2, C, rows, w), F32),
        pltpu.VMEM((tiles // 2, C - 1, rows, w), BF),
        pltpu.VMEM((tiles // 2, C - 1, rows, w), BF),
    ]


def reduce_rows(net, product, scratch, out):
    osend, orecv, ysend, yrecv, sums, zsend, zrecv = scratch
    tiles, C, rows, w = osend.shape
    n = tiles // 2
    k, y = net.k, net.y
    core, over_y = net.core(), net.over_y()
    column = [(1 - y) * n + j for j in range(n)] + [y * n + j for j in range(n)]
    copies = []
    for j in range(tiles):
        osend[j] = product(1 - k, column[j]).astype(BF).reshape(C, rows, w)
        cp = net.remote(osend.at[j], orecv.at[j], net.slot(), core)
        cp.start()
        copies.append(cp)
        yield 1
    ycopies = []
    for j in range(n):
        own = product(k, column[j]).reshape(C, rows, w)
        copies[j].wait_recv()
        ysend[j] = (own + orecv[j].astype(F32)).astype(BF)
        cp = net.remote(ysend.at[j], yrecv.at[j], net.slot(), over_y)
        cp.start()
        ycopies.append(cp)
        yield 1
    zcopies = []
    for j in range(n):
        own = product(k, column[n + j]).reshape(C, rows, w)
        copies[n + j].wait_recv()
        own = own + orecv[n + j].astype(F32)
        sums[j] = own
        ycopies[j].wait_recv()
        sums[j] = sums[j] + yrecv[j].astype(F32)
        for dc in range(1, C):
            to = net.shard(dc)
            zsend[j, dc - 1] = sums[j, to].astype(BF)
            cp = net.remote(zsend.at[j, dc - 1], zrecv.at[j, dc - 1], net.slot(), net.at(c=to))
            cp.start()
            zcopies.append(cp)
        yield 1
    for j in range(n):
        total = sums[j, net.c]
        for dc in range(1, C):
            zcopies[j * (C - 1) + dc - 1].wait_recv()
            total = total + zrecv[j, dc - 1].astype(F32)
        out[j] = total
        yield 1
    for cp in copies + ycopies + zcopies:
        cp.wait_send()
    yield 1


def deal_grads(net, groups):
    C, c, x, k = net.C, net.c, net.x, net.k
    steps = [(dc, dk) for dc in range(C) for dk in range(2)]
    order = steps[1:] + steps[:1]
    over_x = net.over_x()
    xs = {}
    for s in order:
        for g, (grad, pick, xbuf, stage, puts, own_put) in enumerate(groups):
            b = net.shard(s[0]) * 4 + 2 * (1 - x) + (k + s[1]) % 2
            cp = net.remote(grad.at[pick(b)], xbuf.at[2 * s[0] + s[1]], net.slot(), over_x)
            cp.start()
            xs[g, s] = cp
    yield 1
    zs = []
    for s in order:
        tc, tk = net.shard(s[0]), (k + s[1]) % 2
        i = 2 * s[0] + s[1]
        for g, (grad, pick, xbuf, stage, puts, own_put) in enumerate(groups):
            b = tc * 4 + 2 * x + tk
            xs[g, s].wait_recv()
            total = grad[pick(b)].astype(F32) + xbuf[i].astype(F32)
            if s == (0, 0):
                own_put(total)
            else:
                stage[i] = total.astype(BF)
                slot = net.slot()
                for take, put in puts:
                    net.remote(stage.at[(i,) + take], put(c, k), slot, net.at(c=tc, k=tk)).start()
                zs.append((g, s, slot))
        yield 1
    for g, s, slot in zs:
        grad, pick, xbuf, stage, puts, own_put = groups[g]
        i = 2 * s[0] + s[1]
        net.remote(stage.at[i], stage.at[i], slot, over_x).wait()
        yield 1
    for cp in xs.values():
        cp.wait_send()
    yield 1


def half_of(ref, y, width):
    return ref[:, pl.ds(pl.multiple_of(y * width, 128), width)]


def gain_half(gains, y, row, blocks):
    return [gains[y * blocks + i].astype(F32)[row:row + 1] for i in range(blocks)]


def times_gain(value, rows):
    w = value.shape[1] // len(rows)
    return jnp.concatenate([value[:, i * w:(i + 1) * w] * r for i, r in enumerate(rows)], axis=1)


def swap_sums(net, part, out_buf, in_buf):
    out_buf[...] = jnp.broadcast_to(part, out_buf.shape)
    cp = net.remote(out_buf, in_buf, net.slot(), net.over_y())
    cp.start()
    cp.wait()
    return part + in_buf[:, 0:1]


def open_kernel(C, unit, x_ref, g_ref, wq, wk, wv, wo, xg, gains, wqkv, wod, xn, send, recv, loc):
    net = Net(C, send, recv, loc)
    c, x, k = net.c, net.x, net.k
    head = unit
    B = wq.shape[0]
    plane = [(dc, dx, dk) for dc in range(C) for dx in range(2) for dk in range(2)][1:]
    mates = [net.at(c=net.shard(dc), x=(x + dx) % 2, k=(k + dk) % 2) for dc, dx, dk in plane]
    net.meet(mates + [net.over_y()])
    me = c * 4 + 2 * x + k
    own = net.local(g_ref, gains.at[me])
    own.start()
    sent = []
    for (dc, dx, dk), to in zip(plane, mates):
        cp = net.remote(g_ref, gains.at[me], net.slot(), to)
        cp.start()
        sent.append(cp)
    full = slice(None)
    lanes = lambda n, w: pl.ds(pl.multiple_of(n * w, 128), w)
    rows = lambda b: pl.ds(pl.multiple_of(b * B, B), B)
    groups = [
        ([(wq, lambda tc, tk: (full, lanes(2 * tc + tk, head)), lambda b: wqkv.at[rows(b), pl.ds(0, head)]),
          (wk, lambda tc, tk: (full, lanes(tc, head)), lambda b: wqkv.at[rows(b), pl.ds(head, head)]),
          (wv, lambda tc, tk: (full, lanes(tc, head)), lambda b: wqkv.at[rows(b), pl.ds(2 * head, head)])],
         lambda b: wqkv.at[rows(b), :]),
        ([(wo, lambda tc, tk: (pl.ds(pl.multiple_of((2 * tc + tk) * head, head), head), full),
           lambda b: wod.at[:, lanes(b, B)])],
         lambda b: wod.at[:, lanes(b, B)]),
    ]
    weights = deal_weights(net, groups)
    next(weights)
    own.wait()
    for cp in sent:
        cp.wait()
    value = x_ref[...].astype(F32)
    hat = value * lax.rsqrt(jnp.mean(value * value, axis=-1, keepdims=True) + EPS)
    blocks = gains.shape[0]
    xn[...] = times_gain(hat, [gains[b].astype(F32)[0:1] for b in range(blocks)]).astype(BF)
    run(gather_rows(net, xn, xg, False), weights)


def middle_kernel(C, tiles, a_ref, wo_ref, x_ref, gains, cot, wg, wu, wd, hg, cotg, wgu, wdd, h_out, scale_out,
                  red, hn, s_out, s_in, rs, send, recv, loc):
    net = Net(C, send, recv, loc)
    y = net.y
    H = h_out.shape[1]
    B, unit = wg.shape[0], wdd.shape[0]
    w = H * 2 // tiles
    net.meet(net.group() + [net.over_x(), net.over_y()])
    full = slice(None)
    lanes = lambda n, m: pl.ds(pl.multiple_of(n * m, 128), m)
    rows = lambda b: pl.ds(pl.multiple_of(b * B, B), B)
    groups = [
        ([(wg, lambda tc, tk: (full, lanes(2 * tc + tk, unit)), lambda b: wgu.at[rows(b), pl.ds(0, unit)]),
          (wu, lambda tc, tk: (full, lanes(2 * tc + tk, unit)), lambda b: wgu.at[rows(b), pl.ds(unit, unit)])],
         lambda b: wgu.at[rows(b), :]),
        ([(wd, lambda tc, tk: (pl.ds(pl.multiple_of((2 * tc + tk) * unit, 128), unit), full),
           lambda b: wdd.at[:, lanes(b, B)])],
         lambda b: wdd.at[:, lanes(b, B)]),
    ]
    weights = deal_weights(net, groups)
    cots = gather_rows(net, cot, cotg, False)

    def product(kk, tile):
        return jnp.dot(a_ref[kk], wo_ref[:, lanes(tile, w)], preferred_element_type=F32)

    next(cots)
    next(weights)
    run(reduce_rows(net, product, red, rs), weights, cots)
    half = half_of(x_ref, y, H).astype(F32) + jnp.concatenate([rs[j] for j in range(tiles // 2)], axis=1)
    total = swap_sums(net, jnp.sum(half * half, axis=-1, keepdims=True), s_out, s_in)
    scale = lax.rsqrt(total / (2 * H) + EPS)
    h_out[...] = half
    scale_out[...] = jnp.broadcast_to(scale, scale_out.shape)
    hn[...] = times_gain(half * scale, gain_half(gains, y, 1, gains.shape[0] // 2)).astype(BF)
    run(gather_rows(net, hn, hg, True))


def turn_kernel(C, tiles, act, wdd, ggu, wgu, h_ref, scale_ref, gains, cot, ghg, blk, gh_out, part_out,
                red, red2, gb, s_out, s_in, rs, rs2, send, recv, loc):
    net = Net(C, send, recv, loc)
    y = net.y
    H = h_ref.shape[1]
    w = H * 2 // tiles
    net.meet([net.at(c=net.shard(dc)) for dc in range(1, C)] + [net.core(), net.over_y()])
    lanes = lambda n, m: pl.ds(pl.multiple_of(n * m, 128), m)

    def down(kk, tile):
        return jnp.dot(act[kk], wdd[:, lanes(tile, w)], preferred_element_type=F32)

    def normed(kk, tile):
        return lax.dot_general(ggu[kk], wgu[lanes(tile, w), :], NT, preferred_element_type=F32)

    run(reduce_rows(net, normed, red2, rs2), reduce_rows(net, down, red, rs))
    h = h_ref[...]
    blk[y] = (h + jnp.concatenate([rs[j] for j in range(tiles // 2)], axis=1)).astype(BF)
    swap = net.remote(blk.at[y], blk.at[y], net.slot(), net.over_y())
    swap.start()
    g = jnp.concatenate([rs2[j] for j in range(tiles // 2)], axis=1)
    scale = scale_ref[:, 0:1]
    hat = h * scale
    col = jnp.sum(g * hat, axis=0, keepdims=True)
    for i in range(part_out.shape[0]):
        n = part_out.shape[1]
        part_out[i:i + 1] = col[:, i * n:(i + 1) * n]
    m = times_gain(g, gain_half(gains, y, 1, gains.shape[0] // 2))
    mean = swap_sums(net, jnp.sum(m * hat, axis=-1, keepdims=True), s_out, s_in) / (2 * H)
    gh = half_of(cot, y, H).astype(F32) + scale * (m - hat * mean)
    gh_out[...] = gh
    gb[...] = gh.astype(BF)
    run(gather_rows(net, gb, ghg, True))
    swap.wait()


def close_kernel(C, tiles, a_ref, w_ref, x_ref, gains, gh_ref, parts, dgu, dd, dq, do,
                 ig, sums_out, g_out, u_out, d_out, q_out, kv_out, o_out,
                 red, s_out, s_in, rs, xgu, zgu, xd, zd, xq, zq, xo, zo, vec, vin, vx, vz, send, recv, loc):
    net = Net(C, send, recv, loc)
    c, y, k = net.c, net.y, net.k
    H = gh_ref.shape[1]
    w = H * 2 // tiles
    B = g_out.shape[0]
    unit, head = dd.shape[0], do.shape[0]
    net.meet(net.group() + [net.over_x(), net.over_y()])
    full = slice(None)
    lanes = lambda n, m: pl.ds(pl.multiple_of(n * m, 128), m)
    rows = lambda b: (pl.ds(pl.multiple_of(b * B, B), B), full)
    cols = lambda b: (full, lanes(b, B))
    me = 2 * c + k

    def put_gu(v):
        g_out[:, lanes(me, unit)] = v[:, :unit].astype(BF)
        u_out[:, lanes(me, unit)] = v[:, unit:].astype(BF)

    def put_d(v):
        d_out[pl.ds(pl.multiple_of(me * unit, 128), unit), :] = v.astype(BF)

    def put_q(v):
        q_out[:, lanes(me, head)] = v[:, :head].astype(BF)
        kv_out[k, :, lanes(c, head)] = v[:, head:].astype(BF)

    def put_o(v):
        o_out[pl.ds(pl.multiple_of(me * head, 128), head), :] = v.astype(BF)

    groups = [
        (dgu, rows, xgu, zgu,
         [((full, pl.ds(0, unit)), lambda a, b: g_out.at[:, lanes(2 * a + b, unit)]),
          ((full, pl.ds(unit, unit)), lambda a, b: u_out.at[:, lanes(2 * a + b, unit)])], put_gu),
        (dd, cols, xd, zd,
         [((full, full), lambda a, b: d_out.at[pl.ds(pl.multiple_of((2 * a + b) * unit, 128), unit), :])], put_d),
        (dq, rows, xq, zq,
         [((full, pl.ds(0, head)), lambda a, b: q_out.at[:, lanes(2 * a + b, head)]),
          ((full, pl.ds(head, head)), lambda a, b: kv_out.at[b, :, lanes(a, head)])], put_q),
        (do, cols, xo, zo,
         [((full, full), lambda a, b: o_out.at[pl.ds(pl.multiple_of((2 * a + b) * head, 128), head), :])], put_o),
    ]

    def product(kk, tile):
        return lax.dot_general(a_ref[kk], w_ref[lanes(tile, w), :], NT, preferred_element_type=F32)

    grads = deal_grads(net, groups)
    next(grads)
    run(reduce_rows(net, product, red, rs))
    value = x_ref[...].astype(F32)
    scale = lax.rsqrt(jnp.mean(value * value, axis=-1, keepdims=True) + EPS)
    hat = half_of(x_ref, y, H).astype(F32) * scale
    g = jnp.concatenate([rs[j] for j in range(tiles // 2)], axis=1)
    col = jnp.sum(g * hat, axis=0, keepdims=True)
    n = vec.shape[2]
    count = H // n
    vec[0] = parts[...]
    for i in range(count):
        vec[0, i:i + 1] = col[:, i * n:(i + 1) * n]
    first = net.remote(vec.at[0], vin, net.slot(), net.core())
    first.start()
    m = times_gain(g, gain_half(gains, y, 0, gains.shape[0] // 2))
    mean = swap_sums(net, jnp.sum(m * hat, axis=-1, keepdims=True), s_out, s_in) / (2 * H)
    ig[y] = (gh_ref[...] + scale * (m - hat * mean)).astype(BF)
    swap = net.remote(ig.at[y], ig.at[y], net.slot(), net.over_y())
    swap.start()
    first.wait()
    vec[1] = vec[0] + vin[...]
    second = net.remote(vec.at[1], vx, net.slot(), net.over_x())
    second.start()
    second.wait()
    vz[c] = vec[1] + vx[...]
    third = []
    for dc in range(1, C):
        cp = net.remote(vz.at[c], vz.at[c], net.slot(), net.at(c=net.shard(dc)))
        cp.start()
        third.append(cp)
    run(grads)
    for cp in third:
        cp.wait()
    total = vz[0]
    for i in range(1, C):
        total = total + vz[i]
    sums_out[y] = total
    last = net.remote(sums_out.at[y], sums_out.at[y], net.slot(), net.over_y())
    last.start()
    last.wait()
    swap.wait()


def attend_kernel(C, scale, tile, q_ref, kv, qp, kp, o_ref, lse_ref, kvp, m_s, l_s, acc, send, recv, loc):
    net = Net(C, send, recv, loc)
    head = q_ref.shape[1]
    net.meet([net.over_x()])
    swap = net.remote(kv, kvp, 0, net.over_x())
    swap.start()
    steps = q_ref.shape[0] // tile

    def own(i, _):
        r = pl.ds(pl.multiple_of(i * tile, tile), tile)
        s = lax.dot_general(q_ref[r], kv[:, :head], NT, preferred_element_type=F32) * scale
        s = jnp.where(kp[0:1] <= qp[r, 0:1], s, NEG)
        top = jnp.max(s, axis=-1, keepdims=True)
        e = jnp.exp(s - top)
        m_s[r] = jnp.broadcast_to(top, (tile, 128))
        l_s[r] = jnp.broadcast_to(jnp.sum(e, axis=-1, keepdims=True), (tile, 128))
        acc[r] = jnp.dot(e.astype(BF), kv[:, head:], preferred_element_type=F32)
        return 0

    lax.fori_loop(0, steps, own, 0)
    swap.wait()

    @pl.when(net.x == 1)
    def _():
        def more(i, _):
            r = pl.ds(pl.multiple_of(i * tile, tile), tile)
            s = lax.dot_general(q_ref[r], kvp[:, :head], NT, preferred_element_type=F32) * scale
            old = m_s[r, 0:1]
            top = jnp.maximum(old, jnp.max(s, axis=-1, keepdims=True))
            e = jnp.exp(s - top)
            shrink = jnp.exp(old - top)
            m_s[r] = jnp.broadcast_to(top, (tile, 128))
            l_s[r] = jnp.broadcast_to(l_s[r, 0:1] * shrink + jnp.sum(e, axis=-1, keepdims=True), (tile, 128))
            acc[r] = acc[r] * shrink + jnp.dot(e.astype(BF), kvp[:, head:], preferred_element_type=F32)
            return 0

        lax.fori_loop(0, steps, more, 0)

    o_ref[...] = (acc[...] / l_s[...]).astype(BF)
    lse_ref[...] = m_s[...] + jnp.log(l_s[...])


def attend_back_kernel(C, scale, tile, q_ref, kv, kvp, do, lse, delta, qp, kp, dq, kvg, own, peer, cin, xs, xin,
                       send, recv, loc):
    net = Net(C, send, recv, loc)
    head = q_ref.shape[1]
    k = net.k
    net.meet([net.over_x(), net.core()])
    steps = q_ref.shape[0] // tile
    dq[...] = jnp.zeros_like(dq)
    own[...] = jnp.zeros_like(own)

    def sweep(keys, grads, masked):
        def step(i, _):
            r = pl.ds(pl.multiple_of(i * tile, tile), tile)
            q, g = q_ref[r], do[r]
            s = lax.dot_general(keys[:, :head], q, NT, preferred_element_type=F32) * scale
            p = jnp.exp(s - lse[0:1, r])
            if masked:
                p = jnp.where(kp[:, 0:1] <= qp[0:1, r], p, 0.0)
            grads[1] += jnp.dot(p.astype(BF), g, preferred_element_type=F32)
            dp = lax.dot_general(keys[:, head:], g, NT, preferred_element_type=F32)
            ds = (p * (dp - delta[0:1, r])).astype(BF)
            grads[0] += jnp.dot(ds, q, preferred_element_type=F32)
            dq[r] += lax.dot_general(ds, keys[:, :head], TN, preferred_element_type=F32)
            return 0

        lax.fori_loop(0, steps, step, 0)

    one = net.remote(peer.at[1 - k], cin.at[0], net.slot(), net.core())
    two = net.remote(xs, xin, net.slot(), net.over_x())
    three = net.remote(own.at[1 - k], cin.at[1], net.slot(), net.core())

    @pl.when(net.x == 1)
    def _():
        peer[...] = jnp.zeros_like(peer)
        sweep(kvp, peer, False)
        one.start()
        one.wait()
        xs[...] = peer[k] + cin[0]
        two.start()

    sweep(kv, own, True)
    three.start()
    three.wait()
    dq[...] = dq[...] * scale
    kvg[...] = own[k] + cin[1]

    @pl.when(net.x == 1)
    def _():
        two.wait_send()

    @pl.when(net.x == 0)
    def _():
        two.wait_recv()
        kvg[...] = kvg[...] + xin[...]

    @pl.when(k == 0)
    def _():
        kvg[...] = kvg[...] * scale


def call(kernel, name, cid, out_shape, in_specs, out_specs, scratch, *args):
    return pl.pallas_call(
        kernel, name=name, out_shape=out_shape, in_specs=in_specs, out_specs=out_specs,
        scratch_shapes=scratch + [
            pltpu.SemaphoreType.DMA((SLOTS,)), pltpu.SemaphoreType.DMA((SLOTS,)), pltpu.SemaphoreType.DMA((32,)),
        ],
        compiler_params=pltpu.CompilerParams(
            collective_id=cid, has_side_effects=True, vmem_limit_bytes=60 * 1024 * 1024
        ),
    )(*args)


def tensor_parallel(layer_input, block_pair, attn_gain, q_weight, key_projection, value_projection, q_gain, k_gain,
                    o_weight, mlp_gain, gate_weight, up_weight, down_weight, cotangent):
    C = lax.axis_size(CONTEXT)
    R, D = layer_input.shape
    B = q_weight.shape[0]
    NB = 4 * C
    T = 2 * C * R
    H = D // 2
    head = HEAD_SIZE
    unit = gate_weight.shape[1] // (2 * C)
    scale = 1.0 / math.sqrt(head)
    S = jax.ShapeDtypeStruct
    k = lax.axis_index(FSDP) % 2
    x = lax.axis_index(FSDP) // 2
    TILES = 8

    pad = lambda v: jnp.pad(v, (0, B - v.shape[0]))
    packed = jnp.pad(jnp.stack([attn_gain, mlp_gain, pad(q_gain), pad(k_gain)]), ((0, 12), (0, 0)))
    xg, gains, wqkv, wo = call(
        functools.partial(open_kernel, C, head), "open", 1,
        (S((2, C, R, D), BF), S((NB, 16, B), BF), S((D, 3 * head), BF), S((head, D), BF)),
        [VM, VM, HBM, HBM, HBM, HBM], (HBM, VM, HBM, HBM),
        [pltpu.VMEM((R, D), BF)],
        layer_input, packed, q_weight, key_projection, value_projection, o_weight,
    )
    xt = xg.reshape(T, D)
    qgain = gains[:, 2, :q_gain.shape[0]].reshape(head).astype(F32)
    kgain = gains[:, 3, :k_gain.shape[0]].reshape(head).astype(F32)
    order = jnp.arange(T, dtype=jnp.int32)
    ids = (order // R % C) * (4 * R) + x * (2 * R) + (order // (C * R)) * R + order % R
    places = row_places(block_pair, ids, 2 * R)
    cosine, sine = (t[:, 0, :] for t in rope_tables(places, head))
    raw = jnp.dot(xt, wqkv, preferred_element_type=F32)
    q_hat, q_scale = row_norm(raw[:, :head])
    k_hat, k_scale = row_norm(raw[:, head:2 * head])
    q_rot = apply_rotary(q_hat * qgain, cosine, sine).astype(BF)
    k_rot = apply_rotary(k_hat * kgain, cosine, sine).astype(BF)
    kv = jnp.concatenate([k_rot, raw[:, 2 * head:].astype(BF)], axis=1)
    p_col = jnp.broadcast_to(places[:, None], (T, 128))
    p_row = jnp.broadcast_to(places[None, :], (8, T))
    attn_o, lse, kvp = call(
        functools.partial(attend_kernel, C, scale, 256), "attend", 2,
        (S((T, head), BF), S((T, 128), F32), S((T, 2 * head), BF)),
        [VM] * 4, (VM,) * 3,
        [pltpu.VMEM((T, 128), F32), pltpu.VMEM((T, 128), F32), pltpu.VMEM((T, head), F32)],
        q_rot, kv, p_col, p_row,
    )
    red = lambda: reduce_scratch(C, R, D, TILES)
    rs = lambda: pltpu.VMEM((TILES // 2, R, D // TILES), F32)
    stat = lambda: pltpu.VMEM((R, 128), F32)
    hg, cotg, wgu, wd, h_half, h_scale = call(
        lambda *r: middle_kernel(C, TILES, *r[:14], r[14:21], *r[21:]), "middle", 3,
        (S((2, C, R, D), BF), S((2, C, R, D), BF), S((D, 2 * unit), BF), S((unit, D), BF), S((R, H), F32),
         S((R, 128), F32)),
        [VM] * 5 + [HBM] * 3, (HBM, HBM, HBM, HBM, VM, VM),
        red() + [pltpu.VMEM((R, H), BF), stat(), stat(), rs()],
        attn_o.reshape(2, C * R, head), wo, layer_input, gains, cotangent, gate_weight, up_weight, down_weight,
    )
    ht, ct = hg.reshape(T, D), cotg.reshape(T, D)
    gu = jnp.dot(ht, wgu, preferred_element_type=F32)
    gate, up = gu[:, :unit], gu[:, unit:]
    sigma = jax.nn.sigmoid(gate)
    silu = gate * sigma
    act = (silu * up).astype(BF)
    grad_act = jnp.einsum("td,fd->tf", ct, wd, preferred_element_type=F32)
    grad_g = (grad_act * up * (sigma * (1.0 + gate * (1.0 - sigma)))).astype(BF)
    grad_u = (grad_act * silu).astype(BF)
    ggu = jnp.concatenate([grad_g, grad_u], axis=1)
    dd = jnp.einsum("tf,td->fd", act, ct, preferred_element_type=F32).astype(BF)
    dgu = jnp.einsum("tc,tf->cf", ht, ggu, preferred_element_type=F32).astype(BF)
    ghg, blk, gh_half, mlp_part = call(
        lambda *r: turn_kernel(C, TILES, *r[:12], r[12:19], r[19:26], *r[26:]), "turn", 4,
        (S((2, C, R, D), BF), S((2, R, H), BF), S((R, H), F32), S((H // 128, 128), F32)),
        [VM] * 8, (HBM, VM, VM, VM),
        red() + red() + [pltpu.VMEM((R, H), BF), stat(), stat(), rs(), rs()],
        act.reshape(2, C * R, unit), wd, ggu.reshape(2, C * R, 2 * unit), wgu, h_half, h_scale, gains, cotangent,
    )
    gt = ghg.reshape(T, D)
    grad_o = jnp.einsum("td,qd->tq", gt, wo, preferred_element_type=F32).astype(BF)
    do_w = jnp.einsum("tq,td->qd", attn_o, gt, preferred_element_type=F32).astype(BF)
    delta = jnp.sum(grad_o.astype(F32) * attn_o.astype(F32), axis=-1)
    row = lambda v: jnp.broadcast_to(v[None, :], (8, T))
    dq, kvg = call(
        functools.partial(attend_back_kernel, C, scale, 256), "attend_back", 5,
        (S((T, head), F32), S((T, head), F32)),
        [VM] * 8, (VM, VM),
        [pltpu.VMEM((2, T, head), F32), pltpu.VMEM((2, T, head), F32), pltpu.VMEM((2, T, head), F32),
         pltpu.VMEM((T, head), F32), pltpu.VMEM((T, head), F32)],
        q_rot, kv, kvp, grad_o, row(lse[:, 0]), row(delta), p_row, p_col,
    )
    grad_qg = unrotate(dq, cosine, sine)
    q_part = jnp.sum(grad_qg * q_hat, axis=0)
    grad_q = norm_backward(grad_qg * qgain, q_hat, q_scale).astype(BF)
    grad_kg = unrotate(kvg, cosine, sine)
    k_part = jnp.where(k == 0, jnp.sum(grad_kg * k_hat, axis=0), 0.0)
    grad_k = norm_backward(grad_kg * kgain, k_hat, k_scale).astype(BF)
    kv_grad = jnp.where(k == 0, grad_k, kvg.astype(BF))
    gqk = jnp.concatenate([grad_q, kv_grad], axis=1)
    w_kv = jnp.where(k == 0, wqkv[:, head:2 * head], wqkv[:, 2 * head:])
    wqk = jnp.concatenate([wqkv[:, :head], w_kv], axis=1)
    dqk = jnp.einsum("tc,tq->cq", xt, gqk, preferred_element_type=F32).astype(BF)
    n_rows = H // 128
    parts = jnp.concatenate(
        [jnp.zeros_like(mlp_part), mlp_part, q_part[None], k_part[None], jnp.zeros((6, 128), F32)], axis=0
    )
    V = parts.shape
    ig, sums, g_w, u_w, d_w, q_w, kv_w, o_w = call(
        lambda *r: close_kernel(C, TILES, *r[:18], r[18:25], *r[25:]), "close", 6,
        (S((2, R, H), BF), S((2,) + V, F32), S((B, 2 * C * unit), BF), S((B, 2 * C * unit), BF),
         S((2 * C * unit, B), BF), S((B, 2 * C * head), BF), S((2, B, C * head), BF), S((2 * C * head, B), BF)),
        [VM] * 10, (VM,) * 8,
        red() + [stat(), stat(), rs()]
        + [pltpu.VMEM((2 * C, B, 2 * unit), BF)] * 2 + [pltpu.VMEM((2 * C, unit, B), BF)] * 2
        + [pltpu.VMEM((2 * C, B, 2 * head), BF)] * 2 + [pltpu.VMEM((2 * C, head, B), BF)] * 2
        + [pltpu.VMEM((2,) + V, F32), pltpu.VMEM(V, F32), pltpu.VMEM(V, F32), pltpu.VMEM((C,) + V, F32)],
        gqk.reshape(2, C * R, 2 * head), wqk, layer_input, gains, gh_half, parts, dgu, dd, dqk, do_w,
    )
    join = lambda v: jnp.concatenate([v[0], v[1]], axis=1)
    mine = lax.axis_index(CONTEXT) * 4 + lax.axis_index(FSDP)
    both = sums[:, :n_rows].reshape(2 * n_rows, 128)
    both_mlp = sums[:, n_rows:2 * n_rows].reshape(2 * n_rows, 128)
    pick = lambda v: lax.dynamic_slice_in_dim(v.reshape(-1), mine * B, B)
    few = q_gain.shape[0]
    pick_few = lambda v: lax.dynamic_slice_in_dim(v, mine * few, few)
    head_sums = sums[0, 2 * n_rows:] + sums[1, 2 * n_rows:]
    return (
        join(blk), join(ig).astype(F32), pick(both), q_w.astype(F32), kv_w[0].astype(F32), kv_w[1].astype(F32),
        pick_few(head_sums[0]), pick_few(head_sums[1]), o_w.astype(F32), pick(both_mlp), g_w.astype(F32),
        u_w.astype(F32), d_w.astype(F32),
    )


def fits(mesh_shape, layer_input, q_weight, key_projection, gate_weight):
    C = mesh_shape[CONTEXT]
    return (
        mesh_shape[FSDP] == 4 and mesh_shape[HEADS] == 2
        and key_projection.shape[1] == C * HEAD_SIZE and q_weight.shape[1] == 2 * C * HEAD_SIZE
        and gate_weight.shape[1] % (2 * C * 128) == 0 and q_weight.shape[0] == 128
        and layer_input.shape[0] % 128 == 0 and layer_input.shape[1] % (8 * 128) == 0
    )


def solution(mesh):
    def program(*args):
        layer_input, q_weight, key_projection, gate_weight = args[0], args[3], args[4], args[10]
        if fits(dict(mesh.shape), layer_input, q_weight, key_projection, gate_weight):
            return tensor_parallel(*args)
        return per_device(*args)

    return jax.shard_map(
        program,
        mesh=mesh,
        in_specs=(
            P(ROWS, None),
            P(),
            P(ROWS),
            P(ROWS, HEADS),
            P(ROWS, HEADS),
            P(ROWS, HEADS),
            P(ROWS),
            P(ROWS),
            P(HEADS, ROWS),
            P(ROWS),
            P(ROWS, HEADS),
            P(ROWS, HEADS),
            P(HEADS, ROWS),
            P(ROWS, None),
        ),
        out_specs=(
            P(ROWS, None),
            P(ROWS, None),
            P(ROWS),
            P(ROWS, HEADS),
            P(ROWS, HEADS),
            P(ROWS, HEADS),
            P(ROWS),
            P(ROWS),
            P(HEADS, ROWS),
            P(ROWS),
            P(ROWS, HEADS),
            P(ROWS, HEADS),
            P(HEADS, ROWS),
        ),
        check_vma=False,
    )
```

profile of v0, /device:TPU:10, one launch (start us, length us, event | category | flops | bytes accessed | tf_op | source)
XLA Modules:
  0.0 606.8 jit_solution(13419851541246966145)
XLA Ops:
  0.7 0.7 pad_bitcast_fusion
  1.4 1.3 fusion.56.g_ref
  2.7 0.7 select_reduce_fusion
  3.4 0.6 broadcast_in_dim.34.kp.qp
  4.0 1.0 broadcast_in_dim.33.qp.kp
  5.0 61.9 %open.1 = (bf16[2,4,128,2048]{3,2,1,0:T(8,128)(2,1)}, bf16[16,16,128]{2,1,0:T(8,128)(2,1)}, bf16[2048,384]{1,0:T(8,128)(2,1)}, bf16[128,2048]{1,0:T(8,128)(2,1)}) custom-call(bf16[128,2048]{1,0:T(8,128)(2,1)} %r_2_.3, bf16[16,128]{1,0:T(8,128)(2,1)} %fusion.56.g_ref, bf16[128,1024]{1,0:T(8,128)(2,1)} %wq.1, bf16[128,512]{1,0:T(8,128)(2,1)} %wk.1, ...), custom_call_target="tpu_custom_call" | custom-call | tf_op jit(solution)/shard_map/open/pallas_call | solution.py:1036
  66.9 0.0 copy-start.4
  66.9 1.0 convert_reduce_fusion
  67.9 0.1 reshape.296
  68.0 0.1 reshape.295
  68.1 1.5 fusion.62
  69.5 4.5 fusion.64
  74.0 1.1 pad_maximum_fusion.1.r_1_
  75.1 0.3 multiply_reduce_fusion.5
  75.5 0.3 fusion.30
  75.9 2.5 fusion.22
  78.4 1.0 pad_maximum_fusion.2.kv
  79.5 0.8 pad_maximum_fusion.7.q_ref
  80.3 21.8 %attend.1 = (bf16[1024,128]{1,0:T(8,128)(2,1)}, f32[1024,128]{1,0:T(8,128)}, bf16[1024,256]{1,0:T(8,128)(2,1)}) custom-call(bf16[1024,128]{1,0:T(8,128)(2,1)} %pad_maximum_fusion.7.q_ref, bf16[1024,256]{1,0:T(8,128)(2,1)} %pad_maximum_fusion.2.kv, s32[1024,128]{1,0:T(8,128)} %broadcast_in_dim.33.qp.kp, s32[8,1024]{1,0:T(8,128)} %broadcast_in_dim.34.kp.qp), custom_call_target="tpu_custom_call" | custom-call | tf_op jit(solution)/shard_map/attend/pallas_call | solution.py:1036
  102.2 1.2 slice_reduce_fusion
  103.4 0.6 broadcast_in_dim.36.lse
  104.0 150.3 %middle.1 = (bf16[2,4,128,2048]{3,2,1,0:T(8,128)(2,1)}, bf16[2,4,128,2048]{3,2,1,0:T(8,128)(2,1)}, bf16[2048,768]{1,0:T(8,128)(2,1)}, bf16[384,2048]{1,0:T(8,128...) custom-call(bf16[2,512,128]{2,1,0:T(8,128)(2,1)} %bitcast.57, bf16[128,2048]{1,0:T(8,128)(2,1)} %get-tuple-element.44.r_1_, ...), custom_call_target="tpu_custom_call" | custom-call | tf_op jit(solution)/shard_map/middle/pallas_call | solution.py:1036
  254.3 6.3 %fusion.65 = f32[1024,768]{1,0:T(8,128)S(1)} fusion(bf16[1024,2048]{1,0:T(8,128)(2,1)} %bitcast.64, bf16[2048,768]{1,0:T(8,128)(2,1)} %get-tuple-element.46.r_3_), kind=kOutput, calls=%fused_computation.142 | convolution fusion | flops 3221225472 | bytes 10485760 | tf_op jit(solution)/shard_map/dot_general | solution.py:1106
  260.7 2.9 multiply_convert_fusion.1
  263.5 0.0 copy-start.10
  263.6 3.0 convolution_convert_fusion.1.r_7_
  266.5 0.0 copy-done.18
  266.5 15.7 %convolution_convert_fusion.r_6_ = bf16[2048,768]{1,0:T(8,128)(2,1)} fusion(bf16[1024,2048]{1,0:T(8,128)(2,1)S(1)} %bitcast.65, bf16[1024,384]{1,0:T(8,128)(2,1)S(1)} %get-tuple-element.80, bf16[1024,384]{1,0:T(8,128)(2,1)S(1)} %get-tuple-element.79), kind=kOutput, calls=%fused_computation | convolution fusion | flops 3225944064 | bytes 8912896 | tf_op jit(solution)/shard_map/tc,tf->cf/dot_general | solution.py:1116
  282.2 1.3 pad_maximum_fusion
  283.5 108.3 %turn.1 = (bf16[2,4,128,2048]{3,2,1,0:T(8,128)(2,1)}, bf16[2,128,1024]{2,1,0:T(8,128)(2,1)}, f32[128,1024]{1,0:T(8,128)}, f32[8,128]{1,0:T(8,128)}) custom-call(bf16[2,512,384]{2,1,0:T(8,128)(2,1)} %bitcast.58, bf16[384,2048]{1,0:T(8,128)(2,1)} %get-tuple-element.47.r_1_, bf16[2,512,768]{2,1,0:T(8,128)(2,1)} %bitcast.53, ...), custom_call_target="tpu_custom_call" | custom-call | tf_op jit(solution)/shard_map/turn/pallas_call | solution.py:1036
  391.8 4.3 multiply_reduce_fusion.4
  396.2 1.5 convolution_convert_fusion.3.r_9_
  397.7 0.8 pad_maximum_fusion.3
  398.6 0.6 broadcast_in_dim.38.delta
  399.2 23.9 %attend_back.1 = (f32[1024,128]{1,0:T(8,128)}, f32[1024,128]{1,0:T(8,128)}) custom-call(bf16[1024,128]{1,0:T(8,128)(2,1)} %pad_maximum_fusion.7.q_ref, bf16[1024,256]{1,0:T(8,128)(2,1)} %pad_maximum_fusion.2.kv, bf16[1024,256]{1,0:T(8,128)(2,1)} %get-tuple-element.52.kvp, bf16[1024,128]{1,0:T(8,128)(2,1)} %get-tuple-element.109.do, ...), custom_call_target="tpu_custom_call" | custom-call | tf_op jit(solution)/shard_map/attend_back/pallas_call | solution.py:1036
  423.1 4.1 fusion.25
  427.3 0.0 copy-start.1
  427.3 0.0 copy-start.2
  427.3 0.0 copy-start.16
  427.3 0.0 copy-start
  427.3 0.8 copy-done.1
  428.1 0.9 multiply_reduce_fusion
  429.1 0.0 copy-done.16
  429.1 1.8 concatenate.42.r_5_
  430.9 1.8 fusion.31
  432.7 0.5 multiply_convert_fusion.4
  433.2 0.2 copy-done.17
  433.4 2.4 convolution_convert_fusion.2.r_8_
  435.7 0.8 pad_maximum_fusion.6
  436.6 157.4 %close.1 = (bf16[2,128,1024]{2,1,0:T(8,128)(2,1)}, f32[2,24,128]{2,1,0:T(8,128)}, bf16[128,3072]{1,0:T(8,128)(2,1)}, bf16[128,3072]{1,0:T(8,128)(2,1)}, bf16[307...) custom-call(bf16[2,512,256]{2,1,0:T(8,128)(2,1)} %bitcast.56, ...), custom_call_target="tpu_custom_call" | custom-call | tf_op jit(solution)/shard_map/close/pallas_call | solution.py:1036
  594.0 1.1 slice_bitcast_fusion.1
  595.1 0.8 slice_add_fusion
  595.9 0.7 slice_bitcast_fusion.4
  596.6 0.6 dynamic-slice_bitcast_fusion
  597.2 0.6 dynamic-slice_bitcast_fusion.1
  597.8 0.6 dynamic_slice.21
  598.4 0.6 dynamic_slice.16
  598.9 1.1 maximum_convert_fusion
  600.0 0.8 convert_element_type.123
  600.9 0.8 convert_element_type.128
  601.7 0.8 bitcast_convert_fusion
  602.6 1.3 convert_element_type.129
  603.9 1.3 convert_element_type.130
  605.2 1.2 convert_element_type.131
  (43 shorter events, 0.2 us)
Async XLA Ops:
  66.9 2.6 copy-start.4
  254.3 6.3 %copy-start.5 = (bf16[384,2048]{1,0:T(8,128)(2,1)S(1)}, bf16[384,2048]{1,0:T(8,128)(2,1)}, u32[]{:S(2)}) copy-start(bf16[384,2048]{1,0:T(8,128)(2,1)} %get-tuple-element.47.r_1_) | copy-start | bytes 4718596
  254.3 6.3 %copy-start.19 = (bf16[2,4,128,2048]{3,2,1,0:T(8,128)(2,1)S(1)}, bf16[2,4,128,2048]{3,2,1,0:T(8,128)(2,1)}, u32[]{:S(2)}) copy-start(bf16[2,4,128,2048]{3,2,1,0:T(8,128)(2,1)} %get-tuple-element.48) | copy-start | bytes 12582916
  263.5 3.0 copy-start.10
  263.6 3.0 copy-start.18
  283.5 108.3 %copy-start.6 = (bf16[1024,128]{1,0:T(8,128)(2,1)S(1)}, bf16[1024,128]{1,0:T(8,128)(2,1)}, u32[]{:S(2)}) copy-start(bf16[1024,128]{1,0:T(8,128)(2,1)} %get-tuple-element.43) | copy-start | bytes 786436
  283.5 108.3 %copy-start.12 = (bf16[128,2048]{1,0:T(8,128)(2,1)S(1)}, bf16[128,2048]{1,0:T(8,128)(2,1)}, u32[]{:S(2)}) copy-start(bf16[128,2048]{1,0:T(8,128)(2,1)} %get-tuple-element.44.r_1_) | copy-start | bytes 1572868
  391.8 4.3 copy-start.3
  396.2 1.5 copy-start.11
  427.3 0.8 copy-start.1
  427.3 1.7 copy-start.2
  427.3 1.8 copy-start.16
  427.3 3.6 copy-start
  430.9 2.5 copy-start.17
  594.0 6.1 copy-start.15
  594.0 6.9 %copy-start.14 = (bf16[1024,128]{1,0:T(8,128)(2,1)S(1)}, bf16[1024,128]{1,0:T(8,128)(2,1)}, u32[]{:S(2)}) copy-start(bf16[1024,128]{1,0:T(8,128)(2,1)} %get-tuple-element.63) | copy-start | bytes 786436
  594.0 7.7 %copy-start.13 = (bf16[2,128,512]{2,1,0:T(8,128)(2,1)S(1)}, bf16[2,128,512]{2,1,0:T(8,128)(2,1)}, u32[]{:S(2)}) copy-start(bf16[2,128,512]{2,1,0:T(8,128)(2,1)} %get-tuple-element.62) | copy-start | bytes 786436
  595.1 7.4 %copy-start.9 = (bf16[128,3072]{1,0:T(8,128)(2,1)S(1)}, bf16[128,3072]{1,0:T(8,128)(2,1)}, u32[]{:S(2)}) copy-start(bf16[128,3072]{1,0:T(8,128)(2,1)} %get-tuple-element.64) | copy-start | bytes 2359300
  600.9 3.0 copy-start.8
  602.6 2.6 copy-start.7
where the time goes:
time: 614 us; the launch traced here: 607 us
  Pallas kernels  524 us (85%)
  matrix products  40.6 us (7%)
  other arithmetic  29.2 us (5%)
  local copies, waits for them, and re-layouts  12 us (2%)
    pallas_call x6, Pallas kernels, call(): pl.pallas_call(kernel, name=name, out_shape=out_shape, in_specs=in_specs,...  524 us
    dot_general x1, matrix products, tensor_parallel(): jnp.einsum('tc,tf->cf', ht, ggu, preferred_element_type=F32).astype(BF)  15.7 us

commit v1 on v0

--- a/solution.py
+++ b/solution.py
@@ -402,7 +402,7 @@
 MESH = pl.DeviceIdType.MESH
 HBM = pl.BlockSpec(memory_space=pltpu.HBM)
 VM = pl.BlockSpec(memory_space=pltpu.VMEM)
-SLOTS = 160
+SLOTS = 256
 NT = (((1,), (1,)), ((), ()))
 TN = (((0,), (0,)), ((), ()))
 BF = jnp.bfloat16
@@ -560,53 +560,61 @@
     yield 1
 
 
-def deal_weights(net, groups):
-    C, c, x, k = net.C, net.c, net.x, net.k
-    steps = [(dc, dk) for dc in range(C) for dk in range(2)]
-    zs = {(g, s): net.slot() for s in steps for g in range(len(groups))}
-    xs = {(g, s): net.slot() for s in steps for g in range(len(groups))}
-    mine = c * 4 + 2 * x + k
-    keeps = []
-    for s in steps[1:] + steps[:1]:
-        dc, dk = s
-        tc, tk = net.shard(dc), (k + dk) % 2
-        for g, (pieces, whole) in enumerate(groups):
-            for src, pick, put in pieces:
-                if s == (0, 0):
-                    net.remote(src.at[pick(tc, tk)], put(mine), xs[g, s], net.over_x()).start()
-                    keep = net.local(src.at[pick(tc, tk)], put(mine))
-                    keep.start()
-                    keeps.append(keep)
-                else:
-                    net.remote(src.at[pick(tc, tk)], put(mine), zs[g, s], net.at(c=tc, k=tk)).start()
-        if dk:
-            yield 1
-    for s in steps[1:]:
-        dc, dk = s
-        fc, fk = net.shard(-dc), (k + dk) % 2
-        for g, (pieces, whole) in enumerate(groups):
-            block = whole(fc * 4 + 2 * x + fk)
-            net.remote(block, block, zs[g, s], net.over_x()).wait_recv()
-            net.remote(block, block, xs[g, s], net.over_x()).start()
-        yield 1
-    for s in steps:
-        dc, dk = s
-        fc, fk = net.shard(-dc), (k + dk) % 2
-        for g, (pieces, whole) in enumerate(groups):
-            block = whole(fc * 4 + 2 * (1 - x) + fk)
-            net.remote(block, block, xs[g, s], net.over_x()).wait()
-            if s != (0, 0):
-                net.remote(block, block, zs[g, s], net.over_x()).wait_send()
-        yield 1
-    for keep in keeps:
-        keep.wait()
-    yield 1
+class Hand:
+    def __init__(self, net, groups):
+        self.net, self.groups = net, groups
+        self.steps = [(dc, dk) for dc in range(net.C) for dk in range(2)]
+        self.steps = self.steps[1:] + self.steps[:1]
+        self.zs = {(g, s): net.slot() for s in self.steps for g in range(len(groups))}
+        self.xs = {(g, s): net.slot() for s in self.steps for g in range(len(groups))}
+        self.keeps = []
+        self.posted = self.relayed = 0
+
+    def post(self, count):
+        net = self.net
+        mine = net.c * 4 + 2 * net.x + net.k
+        for s in self.steps[self.posted:self.posted + count]:
+            tc, tk = net.shard(s[0]), (net.k + s[1]) % 2
+            for g, (pieces, whole) in enumerate(self.groups):
+                for src, pick, put in pieces:
+                    if s == (0, 0):
+                        net.remote(src.at[pick(tc, tk)], put(mine), self.xs[g, s], net.over_x()).start()
+                        keep = net.local(src.at[pick(tc, tk)], put(mine))
+                        keep.start()
+                        self.keeps.append(keep)
+                    else:
+                        net.remote(src.at[pick(tc, tk)], put(mine), self.zs[g, s], net.at(c=tc, k=tk)).start()
+        self.posted += count
+
+    def block(self, g, s, x):
+        net = self.net
+        return self.groups[g][1](net.shard(-s[0]) * 4 + 2 * x + (net.k + s[1]) % 2)
+
+    def relay(self, count):
+        net = self.net
+        for s in self.steps[self.relayed:min(self.relayed + count, len(self.steps) - 1)]:
+            for g in range(len(self.groups)):
+                block = self.block(g, s, net.x)
+                net.remote(block, block, self.zs[g, s], net.over_x()).wait_recv()
+                net.remote(block, block, self.xs[g, s], net.over_x()).start()
+        self.relayed += count
+
+    def finish(self):
+        net = self.net
+        for s in self.steps:
+            for g in range(len(self.groups)):
+                block = self.block(g, s, 1 - net.x)
+                net.remote(block, block, self.xs[g, s], net.over_x()).wait()
+                if s != (0, 0):
+                    net.remote(block, block, self.zs[g, s], net.over_x()).wait_send()
+        for keep in self.keeps:
+            keep.wait()
 
 
 def reduce_scratch(C, rows, width, tiles):
     w = width // tiles
     return [
-        pltpu.VMEM((tiles, C, rows, w), BF),
+        pltpu.VMEM((tiles // 2, C, rows, w), BF),
         pltpu.VMEM((tiles, C, rows, w), BF),
         pltpu.VMEM((tiles // 2, C, rows, w), BF),
         pltpu.VMEM((tiles // 2, C, rows, w), BF),
@@ -618,15 +626,17 @@
 
 def reduce_rows(net, product, scratch, out):
     osend, orecv, ysend, yrecv, sums, zsend, zrecv = scratch
-    tiles, C, rows, w = osend.shape
+    tiles, C, rows, w = orecv.shape
     n = tiles // 2
     k, y = net.k, net.y
     core, over_y = net.core(), net.over_y()
     column = [(1 - y) * n + j for j in range(n)] + [y * n + j for j in range(n)]
     copies = []
     for j in range(tiles):
-        osend[j] = product(1 - k, column[j]).astype(BF).reshape(C, rows, w)
-        cp = net.remote(osend.at[j], orecv.at[j], net.slot(), core)
+        if j >= n:
+            copies[j - n].wait_send()
+        osend[j % n] = product(1 - k, column[j]).astype(BF).reshape(C, rows, w)
+        cp = net.remote(osend.at[j % n], orecv.at[j], net.slot(), core)
         cp.start()
         copies.append(cp)
         yield 1
@@ -661,47 +671,7 @@
             total = total + zrecv[j, dc - 1].astype(F32)
         out[j] = total
         yield 1
-    for cp in copies + ycopies + zcopies:
-        cp.wait_send()
-    yield 1
-
-
-def deal_grads(net, groups):
-    C, c, x, k = net.C, net.c, net.x, net.k
-    steps = [(dc, dk) for dc in range(C) for dk in range(2)]
-    order = steps[1:] + steps[:1]
-    over_x = net.over_x()
-    xs = {}
-    for s in order:
-        for g, (grad, pick, xbuf, stage, puts, own_put) in enumerate(groups):
-            b = net.shard(s[0]) * 4 + 2 * (1 - x) + (k + s[1]) % 2
-            cp = net.remote(grad.at[pick(b)], xbuf.at[2 * s[0] + s[1]], net.slot(), over_x)
-            cp.start()
-            xs[g, s] = cp
-    yield 1
-    zs = []
-    for s in order:
-        tc, tk = net.shard(s[0]), (k + s[1]) % 2
-        i = 2 * s[0] + s[1]
-        for g, (grad, pick, xbuf, stage, puts, own_put) in enumerate(groups):
-            b = tc * 4 + 2 * x + tk
-            xs[g, s].wait_recv()
-            total = grad[pick(b)].astype(F32) + xbuf[i].astype(F32)
-            if s == (0, 0):
-                own_put(total)
-            else:
-                stage[i] = total.astype(BF)
-                slot = net.slot()
-                for take, put in puts:
-                    net.remote(stage.at[(i,) + take], put(c, k), slot, net.at(c=tc, k=tk)).start()
-                zs.append((g, s, slot))
-        yield 1
-    for g, s, slot in zs:
-        grad, pick, xbuf, stage, puts, own_put = groups[g]
-        i = 2 * s[0] + s[1]
-        net.remote(stage.at[i], stage.at[i], slot, over_x).wait()
-        yield 1
-    for cp in xs.values():
+    for cp in copies[n:] + ycopies + zcopies:
         cp.wait_send()
     yield 1
 
@@ -727,183 +697,503 @@
     return part + in_buf[:, 0:1]
 
 
-def open_kernel(C, unit, x_ref, g_ref, wq, wk, wv, wo, xg, gains, wqkv, wod, xn, send, recv, loc):
+def rotate(value, cosine, sine):
+    return value * cosine + pltpu.roll(value, value.shape[1] // 2, 1) * sine
+
+
+def steps_of(part, count):
+    for _ in range(count):
+        if next(part, 0) == 0:
+            return
+
+
+def front_kernel(C, tiles, head, scale, tile, x_ref, g_ref, cot, qp, kp, cosine, sine, wq, wk, wv, wo, wg, wu, wd,
+                 xg_out, ghg, wqkv, wod, wdd, gains, raw, q_out, kv, kvp, o_out, lse, act, h_out, gh_out, part_out,
+                 g_out, u_out, d_out, zgu, zd,
+                 xn, xg, ht, ct, wgu, m_s, l_s, acc, red, rs, hn, gb, s_out, s_in, s_out2, s_in2, ggu, ggu_t, act_t, from_x, to_x,
+                 send, recv, loc):
     net = Net(C, send, recv, loc)
-    c, x, k = net.c, net.x, net.k
-    head = unit
-    B = wq.shape[0]
+    c, x, y, k = net.c, net.x, net.y, net.k
+    B, unit = wg.shape[0], wdd.shape[0]
+    R, D = x_ref.shape
+    H = D // 2
+    T = 2 * C * R
+    w = D // tiles
+    blocks = gains.shape[0]
     plane = [(dc, dx, dk) for dc in range(C) for dx in range(2) for dk in range(2)][1:]
     mates = [net.at(c=net.shard(dc), x=(x + dx) % 2, k=(k + dk) % 2) for dc, dx, dk in plane]
     net.meet(mates + [net.over_y()])
     me = c * 4 + 2 * x + k
-    own = net.local(g_ref, gains.at[me])
-    own.start()
     sent = []
-    for (dc, dx, dk), to in zip(plane, mates):
+    for to in mates:
         cp = net.remote(g_ref, gains.at[me], net.slot(), to)
         cp.start()
         sent.append(cp)
+    own = net.local(g_ref, gains.at[me])
+    own.start()
     full = slice(None)
-    lanes = lambda n, w: pl.ds(pl.multiple_of(n * w, 128), w)
+    lanes = lambda n, m: pl.ds(pl.multiple_of(n * m, 128), m)
     rows = lambda b: pl.ds(pl.multiple_of(b * B, B), B)
-    groups = [
-        ([(wq, lambda tc, tk: (full, lanes(2 * tc + tk, head)), lambda b: wqkv.at[rows(b), pl.ds(0, head)]),
-          (wk, lambda tc, tk: (full, lanes(tc, head)), lambda b: wqkv.at[rows(b), pl.ds(head, head)]),
-          (wv, lambda tc, tk: (full, lanes(tc, head)), lambda b: wqkv.at[rows(b), pl.ds(2 * head, head)])],
-         lambda b: wqkv.at[rows(b), :]),
-        ([(wo, lambda tc, tk: (pl.ds(pl.multiple_of((2 * tc + tk) * head, head), head), full),
-           lambda b: wod.at[:, lanes(b, B)])],
-         lambda b: wod.at[:, lanes(b, B)]),
-    ]
-    weights = deal_weights(net, groups)
-    next(weights)
+    part = lambda tc, tk, m: pl.ds(pl.multiple_of((2 * tc + tk) * m, 128), m)
+    g_qkv = (
+        [(wq, lambda tc, tk: (full, part(tc, tk, head)), lambda b: wqkv.at[rows(b), pl.ds(0, head)]),
+         (wk, lambda tc, tk: (full, lanes(tc, head)), lambda b: wqkv.at[rows(b), pl.ds(head, head)]),
+         (wv, lambda tc, tk: (full, lanes(tc, head)), lambda b: wqkv.at[rows(b), pl.ds(2 * head, head)])],
+        lambda b: wqkv.at[rows(b), :])
+    g_o = ([(wo, lambda tc, tk: (part(tc, tk, head), full), lambda b: wod.at[:, lanes(b, B)])],
+           lambda b: wod.at[:, lanes(b, B)])
+    g_gu = (
+        [(wg, lambda tc, tk: (full, part(tc, tk, unit)), lambda b: wgu.at[rows(b), pl.ds(0, unit)]),
+         (wu, lambda tc, tk: (full, part(tc, tk, unit)), lambda b: wgu.at[rows(b), pl.ds(unit, unit)])],
+        lambda b: wgu.at[rows(b), :])
+    g_d = ([(wd, lambda tc, tk: (part(tc, tk, unit), full), lambda b: wdd.at[:, lanes(b, B)])],
+           lambda b: wdd.at[:, lanes(b, B)])
+    h_qkv, h_o, h_mlp = Hand(net, [g_qkv]), Hand(net, [g_o]), Hand(net, [g_gu, g_d])
+    every = 2 * C
+    h_qkv.post(4)
     own.wait()
     for cp in sent:
         cp.wait()
     value = x_ref[...].astype(F32)
     hat = value * lax.rsqrt(jnp.mean(value * value, axis=-1, keepdims=True) + EPS)
-    blocks = gains.shape[0]
     xn[...] = times_gain(hat, [gains[b].astype(F32)[0:1] for b in range(blocks)]).astype(BF)
-    run(gather_rows(net, xn, xg, False), weights)
-
-
-def middle_kernel(C, tiles, a_ref, wo_ref, x_ref, gains, cot, wg, wu, wd, hg, cotg, wgu, wdd, h_out, scale_out,
-                  red, hn, s_out, s_in, rs, send, recv, loc):
-    net = Net(C, send, recv, loc)
-    y = net.y
-    H = h_out.shape[1]
-    B, unit = wg.shape[0], wdd.shape[0]
-    w = H * 2 // tiles
-    net.meet(net.group() + [net.over_x(), net.over_y()])
-    full = slice(None)
-    lanes = lambda n, m: pl.ds(pl.multiple_of(n * m, 128), m)
-    rows = lambda b: pl.ds(pl.multiple_of(b * B, B), B)
-    groups = [
-        ([(wg, lambda tc, tk: (full, lanes(2 * tc + tk, unit)), lambda b: wgu.at[rows(b), pl.ds(0, unit)]),
-          (wu, lambda tc, tk: (full, lanes(2 * tc + tk, unit)), lambda b: wgu.at[rows(b), pl.ds(unit, unit)])],
-         lambda b: wgu.at[rows(b), :]),
-        ([(wd, lambda tc, tk: (pl.ds(pl.multiple_of((2 * tc + tk) * unit, 128), unit), full),
-           lambda b: wdd.at[:, lanes(b, B)])],
-         lambda b: wdd.at[:, lanes(b, B)]),
-    ]
-    weights = deal_weights(net, groups)
-    cots = gather_rows(net, cot, cotg, False)
-
-    def product(kk, tile):
-        return jnp.dot(a_ref[kk], wo_ref[:, lanes(tile, w)], preferred_element_type=F32)
-
+    rows_x = gather_rows(net, xn, xg, False)
+    next(rows_x)
+    h_qkv.post(every - 4)
+    for _ in range(C - 1):
+        steps_of(rows_x, 2)
+        h_qkv.relay(2)
+    h_qkv.relay(1)
+    run(rows_x)
+    h_qkv.finish()
+    h_o.post(every)
+    h_mlp.post(every - 1)
+    keep = net.local(xg, xg_out)
+    keep.start()
+    per = tile // R
+    gain_sum = jnp.sum(gains[...].astype(F32), axis=0)
+    qg, kg = gain_sum[2:3], gain_sum[3:4]
+    for kk in range(2):
+        def project(i, _, kk=kk):
+            r = pl.ds(pl.multiple_of(kk * C * R + i * tile, tile), tile)
+            v = jnp.dot(xg[kk, pl.ds(i * per, per)].reshape(tile, D), wqkv[...], preferred_element_type=F32)
+            raw[r] = v[:, :2 * head]
+            cs, sn = cosine[r], sine[r]
+            q = v[:, :head]
+            q = q * lax.rsqrt(jnp.mean(q * q, axis=-1, keepdims=True) + EPS)
+            q_out[r] = rotate(q * qg, cs, sn).astype(BF)
+            key = v[:, head:2 * head]
+            key = key * lax.rsqrt(jnp.mean(key * key, axis=-1, keepdims=True) + EPS)
+            kv[r, 0:head] = rotate(key * kg, cs, sn).astype(BF)
+            kv[r, head:2 * head] = v[:, 2 * head:].astype(BF)
+            return 0
+
+        lax.fori_loop(0, C * R // tile, project, 0)
+    swap = net.remote(kv, kvp, net.slot(), net.over_x())
+    swap.start()
+    h_mlp.post(1)
+
+    def attend(i, _):
+        r = pl.ds(pl.multiple_of(i * tile, tile), tile)
+        s = lax.dot_general(q_out[r], kv[:, :head], NT, preferred_element_type=F32) * scale
+        s = jnp.where(kp[0:1] <= qp[r, 0:1], s, NEG)
+        top = jnp.max(s, axis=-1, keepdims=True)
+        e = jnp.exp(s - top)
+        m_s[r] = jnp.broadcast_to(top, (tile, 128))
+        l_s[r] = jnp.broadcast_to(jnp.sum(e, axis=-1, keepdims=True), (tile, 128))
+        acc[r] = jnp.dot(e.astype(BF), kv[:, head:], preferred_element_type=F32)
+        return 0
+
+    def attend_more(i, _):
+        r = pl.ds(pl.multiple_of(i * tile, tile), tile)
+        s = lax.dot_general(q_out[r], kvp[:, :head], NT, preferred_element_type=F32) * scale
+        old = m_s[r, 0:1]
+        top = jnp.maximum(old, jnp.max(s, axis=-1, keepdims=True))
+        e = jnp.exp(s - top)
+        shrink = jnp.exp(old - top)
+        m_s[r] = jnp.broadcast_to(top, (tile, 128))
+        l_s[r] = jnp.broadcast_to(l_s[r, 0:1] * shrink + jnp.sum(e, axis=-1, keepdims=True), (tile, 128))
+        acc[r] = acc[r] * shrink + jnp.dot(e.astype(BF), kvp[:, head:], preferred_element_type=F32)
+        return 0
+
+    steps = T // tile
+    lax.fori_loop(0, steps, attend, 0)
+    h_o.relay(every - 1)
+    swap.wait()
+
+    @pl.when(x == 1)
+    def _():
+        lax.fori_loop(0, steps, attend_more, 0)
+
+    o_out[...] = (acc[...] / l_s[...]).astype(BF)
+    for i in range(steps):
+        r = pl.ds(i * tile, tile)
+        lse[:, r] = (m_s[r] + jnp.log(l_s[r])).T[0:8]
+    h_o.finish()
+
+    def product(kk, t):
+        return jnp.dot(o_out[pl.ds(pl.multiple_of(kk * C * R, C * R), C * R)], wod[:, lanes(t, w)],
+                       preferred_element_type=F32)
+
+    reduce = reduce_rows(net, product, red, rs)
+    steps_of(reduce, tiles + tiles // 2)
+    h_mlp.relay(2)
+    for _ in range(tiles // 2):
+        steps_of(reduce, 1)
+        h_mlp.relay(1)
+    cots = gather_rows(net, cot, ct, False)
     next(cots)
-    next(weights)
-    run(reduce_rows(net, product, red, rs), weights, cots)
+    h_mlp.relay(every - 3 - tiles // 2)
+    run(reduce)
     half = half_of(x_ref, y, H).astype(F32) + jnp.concatenate([rs[j] for j in range(tiles // 2)], axis=1)
     total = swap_sums(net, jnp.sum(half * half, axis=-1, keepdims=True), s_out, s_in)
-    scale = lax.rsqrt(total / (2 * H) + EPS)
+    hs = lax.rsqrt(total / D + EPS)
     h_out[...] = half
-    scale_out[...] = jnp.broadcast_to(scale, scale_out.shape)
-    hn[...] = times_gain(half * scale, gain_half(gains, y, 1, gains.shape[0] // 2)).astype(BF)
-    run(gather_rows(net, hn, hg, True))
-
-
-def turn_kernel(C, tiles, act, wdd, ggu, wgu, h_ref, scale_ref, gains, cot, ghg, blk, gh_out, part_out,
-                red, red2, gb, s_out, s_in, rs, rs2, send, recv, loc):
-    net = Net(C, send, recv, loc)
-    y = net.y
-    H = h_ref.shape[1]
-    w = H * 2 // tiles
-    net.meet([net.at(c=net.shard(dc)) for dc in range(1, C)] + [net.core(), net.over_y()])
-    lanes = lambda n, m: pl.ds(pl.multiple_of(n * m, 128), m)
-
-    def down(kk, tile):
-        return jnp.dot(act[kk], wdd[:, lanes(tile, w)], preferred_element_type=F32)
-
-    def normed(kk, tile):
-        return lax.dot_general(ggu[kk], wgu[lanes(tile, w), :], NT, preferred_element_type=F32)
-
-    run(reduce_rows(net, normed, red2, rs2), reduce_rows(net, down, red, rs))
-    h = h_ref[...]
-    blk[y] = (h + jnp.concatenate([rs[j] for j in range(tiles // 2)], axis=1)).astype(BF)
-    swap = net.remote(blk.at[y], blk.at[y], net.slot(), net.over_y())
-    swap.start()
-    g = jnp.concatenate([rs2[j] for j in range(tiles // 2)], axis=1)
-    scale = scale_ref[:, 0:1]
-    hat = h * scale
+    hn[...] = times_gain(half * hs, gain_half(gains, y, 1, blocks // 2)).astype(BF)
+    rows_h = gather_rows(net, hn, ht, True)
+    next(rows_h)
+    run(cots, rows_h)
+    h_mlp.finish()
+
+    for kk in range(2):
+        def swiglu(i, _, kk=kk):
+            rr = pl.ds(pl.multiple_of(i * tile, tile), tile)
+            r = pl.ds(pl.multiple_of(kk * C * R + i * tile, tile), tile)
+            gu = jnp.dot(ht[kk, pl.ds(i * per, per)].reshape(tile, D), wgu[...], preferred_element_type=F32)
+            ga = lax.dot_general(ct[kk, pl.ds(i * per, per)].reshape(tile, D), wdd[...], NT,
+                                 preferred_element_type=F32)
+            gate, up = gu[:, :unit], gu[:, unit:]
+            sigma = jax.nn.sigmoid(gate)
+            silu = gate * sigma
+            a = (silu * up).astype(BF)
+            act[kk, rr] = a
+            act_t[:, r] = a.T
+            gg = (ga * up * (sigma * (1.0 + gate * (1.0 - sigma)))).astype(BF)
+            gu = (ga * silu).astype(BF)
+            ggu[kk, rr, 0:unit] = gg
+            ggu[kk, rr, unit:2 * unit] = gu
+            ggu_t[0:unit, r] = gg.T
+            ggu_t[unit:2 * unit, r] = gu.T
+            return 0
+
+        lax.fori_loop(0, C * R // tile, swiglu, 0)
+
+    def normed(kk, t):
+        return lax.dot_general(ggu[kk], wgu[lanes(t, w), :], NT, preferred_element_type=F32)
+
+    pair = 2 * B
+
+    def weight_grads(block, out):
+        t = lanes(block, pair)
+        out(0, 2 * unit, jnp.dot(ggu_t[...], ht[:, :, :, t].reshape(T, pair), preferred_element_type=F32))
+        out(2 * unit, 3 * unit, jnp.dot(act_t[...], ct[:, :, :, t].reshape(T, pair), preferred_element_type=F32))
+
+    swaps = []
+
+    def send_partial(q):
+        def out(a, b, v):
+            to_x[q, a:b] = v.astype(BF)
+
+        weight_grads(net.shard(q + 1) * 2 + 1 - x, out)
+        cp = net.remote(to_x.at[q], from_x.at[q], net.slot(), net.over_x())
+        cp.start()
+        swaps.append(cp)
+
+    place = lambda a, b, m: pl.ds(pl.multiple_of((2 * a + b) * m, 128), m)
+
+    def add_partial(q):
+        dc = (q + 1) % C
+        swaps[q].wait_recv()
+
+        def out(a, b, v):
+            v = v + from_x[q, a:b].astype(F32)
+            for kk in range(2):
+                part = v[:, kk * B:(kk + 1) * B]
+                dk = lax.rem(kk + k, 2)
+                if a:
+                    zd[2 * dc + dk] = part.astype(BF)
+                else:
+                    zgu[2 * dc + dk] = part.T.astype(BF)
+
+        weight_grads(net.shard(dc) * 2 + x, out)
+
+    hand_out = Deal(net, swiglu_groups(g_out, u_out, d_out, zgu, zd, unit))
+    reduce = reduce_rows(net, normed, red, rs)
+    steps_of(reduce, tiles + tiles // 2)
+    for q in range(C):
+        send_partial(q)
+        steps_of(reduce, tiles // 2 // C)
+    add_partial(0)
+    hand_out.post(2)
+    run(reduce)
+    g = jnp.concatenate([rs[j] for j in range(tiles // 2)], axis=1)
+    hat = half * hs
     col = jnp.sum(g * hat, axis=0, keepdims=True)
     for i in range(part_out.shape[0]):
         n = part_out.shape[1]
         part_out[i:i + 1] = col[:, i * n:(i + 1) * n]
-    m = times_gain(g, gain_half(gains, y, 1, gains.shape[0] // 2))
-    mean = swap_sums(net, jnp.sum(m * hat, axis=-1, keepdims=True), s_out, s_in) / (2 * H)
-    gh = half_of(cot, y, H).astype(F32) + scale * (m - hat * mean)
+    m = times_gain(g, gain_half(gains, y, 1, blocks // 2))
+    mean = swap_sums(net, jnp.sum(m * hat, axis=-1, keepdims=True), s_out2, s_in2) / D
+    gh = half_of(cot, y, H).astype(F32) + hs * (m - hat * mean)
     gh_out[...] = gh
     gb[...] = gh.astype(BF)
-    run(gather_rows(net, gb, ghg, True))
-    swap.wait()
-
-
-def close_kernel(C, tiles, a_ref, w_ref, x_ref, gains, gh_ref, parts, dgu, dd, dq, do,
-                 ig, sums_out, g_out, u_out, d_out, q_out, kv_out, o_out,
-                 red, s_out, s_in, rs, xgu, zgu, xd, zd, xq, zq, xo, zo, vec, vin, vx, vz, send, recv, loc):
+    rows_g = gather_rows(net, gb, ghg, True)
+    next(rows_g)
+    add_partial(1)
+    run(rows_g)
+    add_partial(2)
+    add_partial(3)
+    hand_out.finish()
+    for cp in swaps:
+        cp.wait_send()
+    keep.wait()
+
+
+def swiglu_groups(g_out, u_out, d_out, zgu, zd, unit):
+    full = slice(None)
+    place = lambda a, b: pl.ds(pl.multiple_of((2 * a + b) * unit, 128), unit)
+    return [
+        (None, None, None, zgu,
+         [((full, pl.ds(0, unit)), lambda a, b: g_out.at[:, place(a, b)]),
+          ((full, pl.ds(unit, unit)), lambda a, b: u_out.at[:, place(a, b)])], None, False),
+        (None, None, None, zd, [((full, full), lambda a, b: d_out.at[place(a, b), :])], None, False),
+    ]
+
+
+class Deal:
+    def __init__(self, net, groups):
+        self.net, self.groups = net, groups
+        self.order = [(dc, dk) for dc in range(1, net.C) for dk in range(2)] + [(0, 1), (0, 0)]
+        self.xs, self.zs = {}, []
+        self.added = self.posted = 0
+
+    def start(self):
+        net = self.net
+        for s in self.order:
+            b = net.shard(s[0]) * 4 + 2 * (1 - net.x) + (net.k + s[1]) % 2
+            for g, (partial, place, from_x, *_) in enumerate(self.groups):
+                cp = net.remote(partial.at[place(b)], from_x.at[2 * s[0] + s[1]], net.slot(), net.over_x())
+                cp.start()
+                self.xs[g, s] = cp
+
+    def add(self, count):
+        net = self.net
+        for s in self.order[self.added:self.added + count]:
+            i = 2 * s[0] + s[1]
+            b = net.shard(s[0]) * 4 + 2 * net.x + (net.k + s[1]) % 2
+            for g, (partial, place, from_x, sums, puts, keep, flip) in enumerate(self.groups):
+                self.xs[g, s].wait_recv()
+                total = partial[place(b)].astype(F32) + from_x[i].astype(F32)
+                if flip:
+                    total = total.T
+                if s == (0, 0) and keep is not None:
+                    keep(total)
+                else:
+                    sums[i] = total.astype(BF)
+        self.added += count
+
+    def post(self, count):
+        net = self.net
+        for s in self.order[self.posted:min(self.posted + count, len(self.order) - 1)]:
+            i = 2 * s[0] + s[1]
+            to = net.at(c=net.shard(s[0]), k=(net.k + s[1]) % 2)
+            for partial, place, from_x, sums, puts, keep, flip in self.groups:
+                slot = net.slot()
+                for take, put in puts:
+                    net.remote(sums.at[(i,) + take], put(net.c, net.k), slot, to).start()
+                self.zs.append((sums, i, slot))
+        self.posted += count
+
+    def both(self, count):
+        for _ in range(count):
+            self.add(1)
+            self.post(1)
+
+    def finish(self):
+        for sums, i, slot in self.zs:
+            self.net.remote(sums.at[i], sums.at[i], slot, self.net.over_x()).wait()
+        for cp in self.xs.values():
+            cp.wait_send()
+
+
+def back_kernel(C, tiles, head, scale, tile, q_ref, kv, kvp, o_ref, lse, qp, kp, cosine, sine, raw, wqkv, wod, gains,
+                x_ref, gh_ref, h_ref, parts, act, wdd, zgu, zd, g_in, u_in, d_in, ghg, xg,
+                blk, ig, sums_out, g_out, u_out, d_out, q_out, kv_out, o_out,
+                gt, xt, do, delta, dq, own, peer, kvg, cin, xs, xin, gqk, dqk, dow, xq, zq, xo, zo, vec, vin, vx, vz,
+                s_out, s_in, red_d, rs_d, red, rs, send, recv, loc):
     net = Net(C, send, recv, loc)
-    c, y, k = net.c, net.y, net.k
-    H = gh_ref.shape[1]
-    w = H * 2 // tiles
-    B = g_out.shape[0]
-    unit, head = dd.shape[0], do.shape[0]
+    c, x, y, k = net.c, net.x, net.y, net.k
+    T = q_ref.shape[0]
+    R, D = x_ref.shape
+    H = D // 2
+    w = D // tiles
+    blocks = gains.shape[0]
+    load_g = net.local(ghg, gt)
+    load_x = net.local(xg, xt)
+    load_g.start()
+    load_x.start()
+    unit, B = wdd.shape[0], u_out.shape[0]
+    place = lambda a, b, m: pl.ds(pl.multiple_of((2 * a + b) * m, 128), m)
+    g_out[...], u_out[...], d_out[...] = g_in[...], u_in[...], d_in[...]
+    g_out[:, place(c, k, unit)] = zgu[0, :, 0:unit]
+    u_out[:, place(c, k, unit)] = zgu[0, :, unit:2 * unit]
+    d_out[place(c, k, unit), :] = zd[0]
     net.meet(net.group() + [net.over_x(), net.over_y()])
     full = slice(None)
     lanes = lambda n, m: pl.ds(pl.multiple_of(n * m, 128), m)
-    rows = lambda b: (pl.ds(pl.multiple_of(b * B, B), B), full)
-    cols = lambda b: (full, lanes(b, B))
-    me = 2 * c + k
-
-    def put_gu(v):
-        g_out[:, lanes(me, unit)] = v[:, :unit].astype(BF)
-        u_out[:, lanes(me, unit)] = v[:, unit:].astype(BF)
-
-    def put_d(v):
-        d_out[pl.ds(pl.multiple_of(me * unit, 128), unit), :] = v.astype(BF)
-
-    def put_q(v):
-        q_out[:, lanes(me, head)] = v[:, :head].astype(BF)
-        kv_out[k, :, lanes(c, head)] = v[:, head:].astype(BF)
-
-    def put_o(v):
-        o_out[pl.ds(pl.multiple_of(me * head, 128), head), :] = v.astype(BF)
-
-    groups = [
-        (dgu, rows, xgu, zgu,
-         [((full, pl.ds(0, unit)), lambda a, b: g_out.at[:, lanes(2 * a + b, unit)]),
-          ((full, pl.ds(unit, unit)), lambda a, b: u_out.at[:, lanes(2 * a + b, unit)])], put_gu),
-        (dd, cols, xd, zd,
-         [((full, full), lambda a, b: d_out.at[pl.ds(pl.multiple_of((2 * a + b) * unit, 128), unit), :])], put_d),
-        (dq, rows, xq, zq,
-         [((full, pl.ds(0, head)), lambda a, b: q_out.at[:, lanes(2 * a + b, head)]),
-          ((full, pl.ds(head, head)), lambda a, b: kv_out.at[b, :, lanes(a, head)])], put_q),
-        (do, cols, xo, zo,
-         [((full, full), lambda a, b: o_out.at[pl.ds(pl.multiple_of((2 * a + b) * head, 128), head), :])], put_o),
-    ]
-
-    def product(kk, tile):
-        return lax.dot_general(a_ref[kk], w_ref[lanes(tile, w), :], NT, preferred_element_type=F32)
-
-    grads = deal_grads(net, groups)
-    next(grads)
-    run(reduce_rows(net, product, red, rs))
-    value = x_ref[...].astype(F32)
-    scale = lax.rsqrt(jnp.mean(value * value, axis=-1, keepdims=True) + EPS)
-    hat = half_of(x_ref, y, H).astype(F32) * scale
-    g = jnp.concatenate([rs[j] for j in range(tiles // 2)], axis=1)
-    col = jnp.sum(g * hat, axis=0, keepdims=True)
+    deal_u = Deal(net, swiglu_groups(g_out, u_out, d_out, zgu, zd, unit))
+    deal_u.posted = 2
+    deal_u.post(2 * C)
+    steps = T // tile
+    half = T // 2
+
+    def rows_of(i):
+        return pl.ds(pl.multiple_of(i * tile, tile), tile)
+
+    load_g.wait()
+
+    def grad_o(i, _):
+        r = rows_of(i)
+        per = tile // R
+        g = lax.dot_general(gt[i // (steps // 2), pl.ds((i % (steps // 2)) * per, per)].reshape(tile, D), wod[...], NT,
+                            preferred_element_type=F32).astype(BF)
+        do[r] = g
+        d = jnp.sum(g.astype(F32) * o_ref[r].astype(F32), axis=-1, keepdims=True)
+        delta[:, r] = jnp.broadcast_to(d, (tile, 128)).T[0:8]
+        return 0
+
+    lax.fori_loop(0, steps, grad_o, 0)
+    dq[...] = jnp.zeros_like(dq)
+    own[...] = jnp.zeros_like(own)
+
+    def sweep(keys, grads, masked):
+        def step(i, _):
+            r = rows_of(i)
+            q, g = q_ref[r], do[r]
+            s = lax.dot_general(keys[:, :head], q, NT, preferred_element_type=F32) * scale
+            p = jnp.exp(s - lse[0:1, r])
+            if masked:
+                p = jnp.where(kp[:, 0:1] <= qp[0:1, r], p, 0.0)
+            grads[1] += jnp.dot(p.astype(BF), g, preferred_element_type=F32)
+            dp = lax.dot_general(keys[:, head:], g, NT, preferred_element_type=F32)
+            ds = (p * (dp - delta[0:1, r])).astype(BF)
+            grads[0] += jnp.dot(ds, q, preferred_element_type=F32)
+            dq[r] += lax.dot_general(ds, keys[:, :head], TN, preferred_element_type=F32)
+            return 0
+
+        lax.fori_loop(0, steps, step, 0)
+
+    one = net.remote(peer.at[1 - k], cin.at[0], net.slot(), net.core())
+    two = net.remote(xs, xin, net.slot(), net.over_x())
+    three = net.remote(own.at[1 - k], cin.at[1], net.slot(), net.core())
+
+    @pl.when(x == 1)
+    def _():
+        peer[...] = jnp.zeros_like(peer)
+        sweep(kvp, peer, False)
+        one.start()
+        one.wait()
+        xs[...] = peer[k] + cin[0]
+        two.start()
+
+    sweep(kv, own, True)
+    three.start()
+
+    def down(kk, t):
+        return jnp.dot(act[kk], wdd[:, lanes(t, w)], preferred_element_type=F32)
+
+    reduce_d = reduce_rows(net, down, red_d, rs_d)
+    steps_of(reduce_d, tiles + tiles // 2)
+    gain_sum = jnp.sum(gains[...].astype(F32), axis=0)
+    qg, kg = gain_sum[2:3], gain_sum[3:4]
     n = vec.shape[2]
     count = H // n
     vec[0] = parts[...]
+
+    def back_norm(grad, value, gain, r):
+        rotated = grad * cosine[r] - pltpu.roll(grad, head // 2, 1) * sine[r]
+        factor = lax.rsqrt(jnp.mean(value * value, axis=-1, keepdims=True) + EPS)
+        hat = value * factor
+        m = rotated * gain
+        result = factor * (m - hat * jnp.mean(m * hat, axis=-1, keepdims=True))
+        return result, jnp.sum(rotated * hat, axis=0, keepdims=True)
+
+    def finish_q(i, total):
+        r = rows_of(i)
+        g, col = back_norm(dq[r] * scale, raw[r, 0:head], qg, r)
+        gqk[r, 0:head] = g.astype(BF)
+        return total + col
+
+    vec[0, 2 * count:2 * count + 1] = lax.fori_loop(0, steps, finish_q, jnp.zeros((1, head), F32))
+    dow[...] = lax.dot_general(o_ref[...], gt[...].reshape(T, D), TN, preferred_element_type=F32).astype(BF)
+    three.wait()
+    kvg[...] = own[k] + cin[1]
+
+    @pl.when(x == 1)
+    def _():
+        two.wait_send()
+
+    @pl.when(x == 0)
+    def _():
+        two.wait_recv()
+        kvg[...] = kvg[...] + xin[...]
+
+    def finish_kv(i, total):
+        r = rows_of(i)
+        v = kvg[r]
+        g, col = back_norm(v * scale, raw[r, head:2 * head], kg, r)
+        gqk[r, head:2 * head] = jnp.where(k == 0, g, v).astype(BF)
+        return total + jnp.where(k == 0, col, 0.0)
+
+    vec[0, 2 * count + 1:2 * count + 2] = lax.fori_loop(0, steps, finish_kv, jnp.zeros((1, head), F32))
+
+    def product(kk, t):
+        r = pl.ds(pl.multiple_of(kk * half, half), half)
+        a = lax.dot_general(gqk[r, 0:head], wqkv[lanes(t, w), 0:head], NT, preferred_element_type=F32)
+        return a + lax.dot_general(gqk[r, head:2 * head], wqkv[lanes(t, w), lanes(1 + k, head)], NT,
+                                   preferred_element_type=F32)
+
+    def keep_q(v):
+        q_out[:, place(c, k, head)] = v[:, :head].astype(BF)
+        kv_out[k, :, lanes(c, head)] = v[:, head:].astype(BF)
+
+    def keep_o(v):
+        o_out[place(c, k, head), :] = v.astype(BF)
+
+    deal_q = Deal(net, [
+        (dqk, lambda b: (full, lanes(b, B)), xq, zq,
+         [((full, pl.ds(0, head)), lambda a, b: q_out.at[:, place(a, b, head)]),
+          ((full, pl.ds(head, head)), lambda a, b: kv_out.at[b, :, lanes(a, head)])], keep_q, True),
+        (dow, lambda b: (full, lanes(b, B)), xo, zo,
+         [((full, full), lambda a, b: o_out.at[place(a, b, head), :])], keep_o, False),
+    ])
+    reduce = reduce_rows(net, product, red, rs)
+    steps_of(reduce, tiles + tiles // 2)
+    load_x.wait()
+    for i in range(tiles):
+        t = pl.ds(i * w, w)
+        dqk[:, t] = lax.dot_general(gqk[...], xt[:, :, :, t].reshape(T, w), TN, preferred_element_type=F32).astype(BF)
+    deal_q.start()
+    steps_of(reduce_d, tiles // 2)
+    steps_of(reduce, tiles // 2)
+    deal_q.both(2 * C)
+    run(reduce_d)
+    blk[y] = (h_ref[...] + jnp.concatenate([rs_d[j] for j in range(tiles // 2)], axis=1)).astype(BF)
+    swap_b = net.remote(blk.at[y], blk.at[y], net.slot(), net.over_y())
+    swap_b.start()
+    run(reduce)
+    value = x_ref[...].astype(F32)
+    xscale = lax.rsqrt(jnp.mean(value * value, axis=-1, keepdims=True) + EPS)
+    hat = half_of(x_ref, y, H).astype(F32) * xscale
+    g = jnp.concatenate([rs[j] for j in range(tiles // 2)], axis=1)
+    col = jnp.sum(g * hat, axis=0, keepdims=True)
     for i in range(count):
         vec[0, i:i + 1] = col[:, i * n:(i + 1) * n]
     first = net.remote(vec.at[0], vin, net.slot(), net.core())
     first.start()
-    m = times_gain(g, gain_half(gains, y, 0, gains.shape[0] // 2))
-    mean = swap_sums(net, jnp.sum(m * hat, axis=-1, keepdims=True), s_out, s_in) / (2 * H)
-    ig[y] = (gh_ref[...] + scale * (m - hat * mean)).astype(BF)
+    m = times_gain(g, gain_half(gains, y, 0, blocks // 2))
+    mean = swap_sums(net, jnp.sum(m * hat, axis=-1, keepdims=True), s_out, s_in) / D
+    ig[y] = (gh_ref[...] + xscale * (m - hat * mean)).astype(BF)
     swap = net.remote(ig.at[y], ig.at[y], net.slot(), net.over_y())
     swap.start()
     first.wait()
@@ -917,7 +1207,6 @@
         cp = net.remote(vz.at[c], vz.at[c], net.slot(), net.at(c=net.shard(dc)))
         cp.start()
         third.append(cp)
-    run(grads)
     for cp in third:
         cp.wait()
     total = vz[0]
@@ -926,110 +1215,11 @@
     sums_out[y] = total
     last = net.remote(sums_out.at[y], sums_out.at[y], net.slot(), net.over_y())
     last.start()
+    deal_u.finish()
+    deal_q.finish()
     last.wait()
     swap.wait()
-
-
-def attend_kernel(C, scale, tile, q_ref, kv, qp, kp, o_ref, lse_ref, kvp, m_s, l_s, acc, send, recv, loc):
-    net = Net(C, send, recv, loc)
-    head = q_ref.shape[1]
-    net.meet([net.over_x()])
-    swap = net.remote(kv, kvp, 0, net.over_x())
-    swap.start()
-    steps = q_ref.shape[0] // tile
-
-    def own(i, _):
-        r = pl.ds(pl.multiple_of(i * tile, tile), tile)
-        s = lax.dot_general(q_ref[r], kv[:, :head], NT, preferred_element_type=F32) * scale
-        s = jnp.where(kp[0:1] <= qp[r, 0:1], s, NEG)
-        top = jnp.max(s, axis=-1, keepdims=True)
-        e = jnp.exp(s - top)
-        m_s[r] = jnp.broadcast_to(top, (tile, 128))
-        l_s[r] = jnp.broadcast_to(jnp.sum(e, axis=-1, keepdims=True), (tile, 128))
-        acc[r] = jnp.dot(e.astype(BF), kv[:, head:], preferred_element_type=F32)
-        return 0
-
-    lax.fori_loop(0, steps, own, 0)
-    swap.wait()
-
-    @pl.when(net.x == 1)
-    def _():
-        def more(i, _):
-            r = pl.ds(pl.multiple_of(i * tile, tile), tile)
-            s = lax.dot_general(q_ref[r], kvp[:, :head], NT, preferred_element_type=F32) * scale
-            old = m_s[r, 0:1]
-            top = jnp.maximum(old, jnp.max(s, axis=-1, keepdims=True))
-            e = jnp.exp(s - top)
-            shrink = jnp.exp(old - top)
-            m_s[r] = jnp.broadcast_to(top, (tile, 128))
-            l_s[r] = jnp.broadcast_to(l_s[r, 0:1] * shrink + jnp.sum(e, axis=-1, keepdims=True), (tile, 128))
-            acc[r] = acc[r] * shrink + jnp.dot(e.astype(BF), kvp[:, head:], preferred_element_type=F32)
-            return 0
-
-        lax.fori_loop(0, steps, more, 0)
-
-    o_ref[...] = (acc[...] / l_s[...]).astype(BF)
-    lse_ref[...] = m_s[...] + jnp.log(l_s[...])
-
-
-def attend_back_kernel(C, scale, tile, q_ref, kv, kvp, do, lse, delta, qp, kp, dq, kvg, own, peer, cin, xs, xin,
-                       send, recv, loc):
-    net = Net(C, send, recv, loc)
-    head = q_ref.shape[1]
-    k = net.k
-    net.meet([net.over_x(), net.core()])
-    steps = q_ref.shape[0] // tile
-    dq[...] = jnp.zeros_like(dq)
-    own[...] = jnp.zeros_like(own)
-
-    def sweep(keys, grads, masked):
-        def step(i, _):
-            r = pl.ds(pl.multiple_of(i * tile, tile), tile)
-            q, g = q_ref[r], do[r]
-            s = lax.dot_general(keys[:, :head], q, NT, preferred_element_type=F32) * scale
-            p = jnp.exp(s - lse[0:1, r])
-            if masked:
-                p = jnp.where(kp[:, 0:1] <= qp[0:1, r], p, 0.0)
-            grads[1] += jnp.dot(p.astype(BF), g, preferred_element_type=F32)
-            dp = lax.dot_general(keys[:, head:], g, NT, preferred_element_type=F32)
-            ds = (p * (dp - delta[0:1, r])).astype(BF)
-            grads[0] += jnp.dot(ds, q, preferred_element_type=F32)
-            dq[r] += lax.dot_general(ds, keys[:, :head], TN, preferred_element_type=F32)
-            return 0
-
-        lax.fori_loop(0, steps, step, 0)
-
-    one = net.remote(peer.at[1 - k], cin.at[0], net.slot(), net.core())
-    two = net.remote(xs, xin, net.slot(), net.over_x())
-    three = net.remote(own.at[1 - k], cin.at[1], net.slot(), net.core())
-
-    @pl.when(net.x == 1)
-    def _():
-        peer[...] = jnp.zeros_like(peer)
-        sweep(kvp, peer, False)
-        one.start()
-        one.wait()
-        xs[...] = peer[k] + cin[0]
-        two.start()
-
-    sweep(kv, own, True)
-    three.start()
-    three.wait()
-    dq[...] = dq[...] * scale
-    kvg[...] = own[k] + cin[1]
-
-    @pl.when(net.x == 1)
-    def _():
-        two.wait_send()
-
-    @pl.when(net.x == 0)
-    def _():
-        two.wait_recv()
-        kvg[...] = kvg[...] + xin[...]
-
-    @pl.when(k == 0)
-    def _():
-        kvg[...] = kvg[...] * scale
+    swap_b.wait()
 
 
 def call(kernel, name, cid, out_shape, in_specs, out_specs, scratch, *args):
@@ -1055,114 +1245,63 @@
     head = HEAD_SIZE
     unit = gate_weight.shape[1] // (2 * C)
     scale = 1.0 / math.sqrt(head)
+    half = head // 2
     S = jax.ShapeDtypeStruct
     k = lax.axis_index(FSDP) % 2
     x = lax.axis_index(FSDP) // 2
     TILES = 8
 
-    pad = lambda v: jnp.pad(v, (0, B - v.shape[0]))
-    packed = jnp.pad(jnp.stack([attn_gain, mlp_gain, pad(q_gain), pad(k_gain)]), ((0, 12), (0, 0)))
-    xg, gains, wqkv, wo = call(
-        functools.partial(open_kernel, C, head), "open", 1,
-        (S((2, C, R, D), BF), S((NB, 16, B), BF), S((D, 3 * head), BF), S((head, D), BF)),
-        [VM, VM, HBM, HBM, HBM, HBM], (HBM, VM, HBM, HBM),
-        [pltpu.VMEM((R, D), BF)],
-        layer_input, packed, q_weight, key_projection, value_projection, o_weight,
-    )
-    xt = xg.reshape(T, D)
-    qgain = gains[:, 2, :q_gain.shape[0]].reshape(head).astype(F32)
-    kgain = gains[:, 3, :k_gain.shape[0]].reshape(head).astype(F32)
+    red = lambda: reduce_scratch(C, R, D, TILES)
+    rs = lambda: pltpu.VMEM((TILES // 2, R, D // TILES), F32)
+    stat = lambda: pltpu.VMEM((R, 128), F32)
+    mine = lax.axis_index(CONTEXT) * 4 + lax.axis_index(FSDP)
+    spread = lambda v: lax.dynamic_update_slice_in_dim(jnp.zeros((head,), BF), v, mine * v.shape[0], 0)
+    packed = jnp.pad(jnp.stack([attn_gain, mlp_gain, spread(q_gain), spread(k_gain)]), ((0, 12), (0, 0)))
     order = jnp.arange(T, dtype=jnp.int32)
     ids = (order // R % C) * (4 * R) + x * (2 * R) + (order // (C * R)) * R + order % R
     places = row_places(block_pair, ids, 2 * R)
     cosine, sine = (t[:, 0, :] for t in rope_tables(places, head))
-    raw = jnp.dot(xt, wqkv, preferred_element_type=F32)
-    q_hat, q_scale = row_norm(raw[:, :head])
-    k_hat, k_scale = row_norm(raw[:, head:2 * head])
-    q_rot = apply_rotary(q_hat * qgain, cosine, sine).astype(BF)
-    k_rot = apply_rotary(k_hat * kgain, cosine, sine).astype(BF)
-    kv = jnp.concatenate([k_rot, raw[:, 2 * head:].astype(BF)], axis=1)
+    cosine = jnp.concatenate([cosine, cosine], axis=1)
+    sine = jnp.concatenate([-sine, sine], axis=1)
     p_col = jnp.broadcast_to(places[:, None], (T, 128))
     p_row = jnp.broadcast_to(places[None, :], (8, T))
-    attn_o, lse, kvp = call(
-        functools.partial(attend_kernel, C, scale, 256), "attend", 2,
-        (S((T, head), BF), S((T, 128), F32), S((T, 2 * head), BF)),
-        [VM] * 4, (VM,) * 3,
-        [pltpu.VMEM((T, 128), F32), pltpu.VMEM((T, 128), F32), pltpu.VMEM((T, head), F32)],
-        q_rot, kv, p_col, p_row,
-    )
-    red = lambda: reduce_scratch(C, R, D, TILES)
-    rs = lambda: pltpu.VMEM((TILES // 2, R, D // TILES), F32)
-    stat = lambda: pltpu.VMEM((R, 128), F32)
-    hg, cotg, wgu, wd, h_half, h_scale = call(
-        lambda *r: middle_kernel(C, TILES, *r[:14], r[14:21], *r[21:]), "middle", 3,
-        (S((2, C, R, D), BF), S((2, C, R, D), BF), S((D, 2 * unit), BF), S((unit, D), BF), S((R, H), F32),
-         S((R, 128), F32)),
-        [VM] * 5 + [HBM] * 3, (HBM, HBM, HBM, HBM, VM, VM),
-        red() + [pltpu.VMEM((R, H), BF), stat(), stat(), rs()],
-        attn_o.reshape(2, C * R, head), wo, layer_input, gains, cotangent, gate_weight, up_weight, down_weight,
-    )
-    ht, ct = hg.reshape(T, D), cotg.reshape(T, D)
-    gu = jnp.dot(ht, wgu, preferred_element_type=F32)
-    gate, up = gu[:, :unit], gu[:, unit:]
-    sigma = jax.nn.sigmoid(gate)
-    silu = gate * sigma
-    act = (silu * up).astype(BF)
-    grad_act = jnp.einsum("td,fd->tf", ct, wd, preferred_element_type=F32)
-    grad_g = (grad_act * up * (sigma * (1.0 + gate * (1.0 - sigma)))).astype(BF)
-    grad_u = (grad_act * silu).astype(BF)
-    ggu = jnp.concatenate([grad_g, grad_u], axis=1)
-    dd = jnp.einsum("tf,td->fd", act, ct, preferred_element_type=F32).astype(BF)
-    dgu = jnp.einsum("tc,tf->cf", ht, ggu, preferred_element_type=F32).astype(BF)
-    ghg, blk, gh_half, mlp_part = call(
-        lambda *r: turn_kernel(C, TILES, *r[:12], r[12:19], r[19:26], *r[26:]), "turn", 4,
-        (S((2, C, R, D), BF), S((2, R, H), BF), S((R, H), F32), S((H // 128, 128), F32)),
-        [VM] * 8, (HBM, VM, VM, VM),
-        red() + red() + [pltpu.VMEM((R, H), BF), stat(), stat(), rs(), rs()],
-        act.reshape(2, C * R, unit), wd, ggu.reshape(2, C * R, 2 * unit), wgu, h_half, h_scale, gains, cotangent,
-    )
-    gt = ghg.reshape(T, D)
-    grad_o = jnp.einsum("td,qd->tq", gt, wo, preferred_element_type=F32).astype(BF)
-    do_w = jnp.einsum("tq,td->qd", attn_o, gt, preferred_element_type=F32).astype(BF)
-    delta = jnp.sum(grad_o.astype(F32) * attn_o.astype(F32), axis=-1)
-    row = lambda v: jnp.broadcast_to(v[None, :], (8, T))
-    dq, kvg = call(
-        functools.partial(attend_back_kernel, C, scale, 256), "attend_back", 5,
-        (S((T, head), F32), S((T, head), F32)),
-        [VM] * 8, (VM, VM),
-        [pltpu.VMEM((2, T, head), F32), pltpu.VMEM((2, T, head), F32), pltpu.VMEM((2, T, head), F32),
-         pltpu.VMEM((T, head), F32), pltpu.VMEM((T, head), F32)],
-        q_rot, kv, kvp, grad_o, row(lse[:, 0]), row(delta), p_row, p_col,
-    )
-    grad_qg = unrotate(dq, cosine, sine)
-    q_part = jnp.sum(grad_qg * q_hat, axis=0)
-    grad_q = norm_backward(grad_qg * qgain, q_hat, q_scale).astype(BF)
-    grad_kg = unrotate(kvg, cosine, sine)
-    k_part = jnp.where(k == 0, jnp.sum(grad_kg * k_hat, axis=0), 0.0)
-    grad_k = norm_backward(grad_kg * kgain, k_hat, k_scale).astype(BF)
-    kv_grad = jnp.where(k == 0, grad_k, kvg.astype(BF))
-    gqk = jnp.concatenate([grad_q, kv_grad], axis=1)
-    w_kv = jnp.where(k == 0, wqkv[:, head:2 * head], wqkv[:, 2 * head:])
-    wqk = jnp.concatenate([wqkv[:, :head], w_kv], axis=1)
-    dqk = jnp.einsum("tc,tq->cq", xt, gqk, preferred_element_type=F32).astype(BF)
+    vm = lambda *shape: pltpu.VMEM(shape, BF)
+    (xg, ghg, wqkv, wo, wd, gains, raw, q_rot, kv, kvp, attn_o, lse, act, h_half, gh_half, mlp_part, g_in, u_in, d_in,
+     zgu, zd) = call(
+        lambda *r: front_kernel(C, TILES, head, scale, 256, *r[:43], r[43:50], *r[50:]), "front", 1,
+        (S((2, C, R, D), BF), S((2, C, R, D), BF), S((D, 3 * head), BF), S((head, D), BF), S((unit, D), BF),
+         S((NB, 16, B), BF), S((T, 2 * head), F32), S((T, head), BF), S((T, 2 * head), BF), S((T, 2 * head), BF),
+         S((T, head), BF), S((8, T), F32), S((2, C * R, unit), BF), S((R, H), F32), S((R, H), F32),
+         S((H // 128, 128), F32), S((B, 2 * C * unit), BF), S((B, 2 * C * unit), BF), S((2 * C * unit, B), BF),
+         S((2 * C, B, 2 * unit), BF), S((2 * C, unit, B), BF)),
+        [VM] * 7 + [HBM] * 7, (HBM,) * 2 + (VM,) * 19,
+        [vm(R, D), vm(2, C, R, D), vm(2, C, R, D), vm(2, C, R, D), vm(D, 2 * unit), pltpu.VMEM((T, 128), F32),
+         pltpu.VMEM((T, 128), F32), pltpu.VMEM((T, head), F32)] + red()
+        + [rs(), vm(R, H), vm(R, H), stat(), stat(), stat(), stat(), vm(2, C * R, 2 * unit), vm(2 * unit, T),
+           vm(unit, T), vm(C, 3 * unit, 2 * B), vm(C, 3 * unit, 2 * B)],
+        layer_input, packed, cotangent, p_col, p_row, cosine, sine,
+        q_weight, key_projection, value_projection, o_weight, gate_weight, up_weight, down_weight,
+    )
     n_rows = H // 128
-    parts = jnp.concatenate(
-        [jnp.zeros_like(mlp_part), mlp_part, q_part[None], k_part[None], jnp.zeros((6, 128), F32)], axis=0
-    )
+    parts = jnp.concatenate([jnp.zeros_like(mlp_part), mlp_part, jnp.zeros((8, 128), F32)], axis=0)
     V = parts.shape
-    ig, sums, g_w, u_w, d_w, q_w, kv_w, o_w = call(
-        lambda *r: close_kernel(C, TILES, *r[:18], r[18:25], *r[25:]), "close", 6,
-        (S((2, R, H), BF), S((2,) + V, F32), S((B, 2 * C * unit), BF), S((B, 2 * C * unit), BF),
+    wide = lambda: pltpu.VMEM((2, T, head), F32)
+    one = lambda: pltpu.VMEM((T, head), F32)
+    blk, ig, sums, g_w, u_w, d_w, q_w, kv_w, o_w = call(
+        lambda *r: back_kernel(C, TILES, head, scale, 256, *r[:59], r[59:66], r[66], r[67:74], *r[74:]), "back", 3,
+        (S((2, R, H), BF), S((2, R, H), BF), S((2,) + V, F32), S((B, 2 * C * unit), BF), S((B, 2 * C * unit), BF),
          S((2 * C * unit, B), BF), S((B, 2 * C * head), BF), S((2, B, C * head), BF), S((2 * C * head, B), BF)),
-        [VM] * 10, (VM,) * 8,
-        red() + [stat(), stat(), rs()]
-        + [pltpu.VMEM((2 * C, B, 2 * unit), BF)] * 2 + [pltpu.VMEM((2 * C, unit, B), BF)] * 2
-        + [pltpu.VMEM((2 * C, B, 2 * head), BF)] * 2 + [pltpu.VMEM((2 * C, head, B), BF)] * 2
-        + [pltpu.VMEM((2,) + V, F32), pltpu.VMEM(V, F32), pltpu.VMEM(V, F32), pltpu.VMEM((C,) + V, F32)],
-        gqk.reshape(2, C * R, 2 * head), wqk, layer_input, gains, gh_half, parts, dgu, dd, dqk, do_w,
+        [VM] * 24 + [HBM] * 2, (VM,) * 9,
+        [pltpu.VMEM((2, C, R, D), BF), pltpu.VMEM((2, C, R, D), BF), pltpu.VMEM((T, head), BF), pltpu.VMEM((8, T), F32),
+         one(), wide(), wide(), one(), wide(), one(), one(), pltpu.VMEM((T, 2 * head), BF),
+         pltpu.VMEM((2 * head, D), BF), pltpu.VMEM((head, D), BF), pltpu.VMEM((2 * C, 2 * head, B), BF),
+         pltpu.VMEM((2 * C, B, 2 * head), BF), pltpu.VMEM((2 * C, head, B), BF), pltpu.VMEM((2 * C, head, B), BF),
+         pltpu.VMEM((2,) + V, F32), pltpu.VMEM(V, F32), pltpu.VMEM(V, F32), pltpu.VMEM((C,) + V, F32), stat(), stat()]
+        + red() + [rs()] + red() + [rs()],
+        q_rot, kv, kvp, attn_o, lse, p_row, p_col, cosine, sine, raw, wqkv, wo, gains, layer_input, gh_half, h_half,
+        parts, act, wd, zgu, zd, g_in, u_in, d_in, ghg, xg,
     )
     join = lambda v: jnp.concatenate([v[0], v[1]], axis=1)
-    mine = lax.axis_index(CONTEXT) * 4 + lax.axis_index(FSDP)
     both = sums[:, :n_rows].reshape(2 * n_rows, 128)
     both_mlp = sums[:, n_rows:2 * n_rows].reshape(2 * n_rows, 128)
     pick = lambda v: lax.dynamic_slice_in_dim(v.reshape(-1), mine * B, B)

time: 614 us -> 425 us (0.69)
  the two profiles are of different devices: /device:TPU:10 before, /device:TPU:0 now
where the time goes in v1:
time: 425 us; the launch traced here: 417 us
  Pallas kernels  394 us (93%)
  other arithmetic  15.5 us (4%)
  local copies, waits for them, and re-layouts  6.22 us (1%)
    pallas_call x2, Pallas kernels, call(): pl.pallas_call(kernel, name=name, out_shape=out_shape, in_specs=in_specs,...  394 us

profile of v1, /device:TPU:0, one launch (start us, length us, event | category | flops | bytes accessed | tf_op | source)
XLA Modules:
  0.0 417.2 jit_solution(16528523038714590067)
XLA Ops:
  0.7 0.8 dynamic_update_slice.9
  1.5 0.8 dynamic_update_slice.8
  2.2 1.3 fusion.25.r_1_
  3.5 0.7 select_reduce_fusion
  4.3 0.6 broadcast_in_dim.19.r_4_.r_5_
  4.9 1.0 broadcast_in_dim.18.r_3_.r_6_
  5.9 1.9 fusion
  7.8 1.0 pad_maximum_fusion.1.r_6_.r_8_
  8.8 1.0 pad_maximum_fusion.r_5_.r_7_
  9.8 271.4 %front.1 = (bf16[2,4,128,2048]{3,2,1,0:T(8,128)(2,1)}, bf16[2,4,128,2048]{3,2,1,0:T(8,128)(2,1)}, bf16[2048,384]{1,0:T(8,128)(2,1)}, bf16[128,2048]{1,0:T(8,128)...) custom-call(bf16[128,2048]{1,0:T(8,128)(2,1)} %r_13_.3, ...), custom_call_target="tpu_custom_call" | custom-call | tf_op jit(solution)/shard_map/front/pallas_call | solution.py:1226
  281.3 1.3 pad_maximum_fusion.3.r_16_
  282.6 122.8 %back.1 = (bf16[2,128,1024]{2,1,0:T(8,128)(2,1)}, bf16[2,128,1024]{2,1,0:T(8,128)(2,1)}, f32[2,24,128]{2,1,0:T(8,128)}, bf16[128,3072]{1,0:T(8,128)(2,1)}, bf16[...) custom-call(bf16[1024,128]{1,0:T(8,128)(2,1)} %get-tuple-element.43., ...), custom_call_target="tpu_custom_call" | custom-call | tf_op jit(solution)/shard_map/back/pallas_call | solution.py:1226
  405.4 0.0 copy-start.6
  405.4 1.3 slice_bitcast_fusion.1
  406.7 0.0 copy-start.5
  406.7 0.0 copy-done.6
  406.7 0.6 dynamic-slice_bitcast_fusion
  407.3 0.6 dynamic_slice.21
  407.9 0.6 dynamic_slice.16
  408.5 0.0 copy-start.4
  408.5 1.1 maximum_convert_fusion
  409.6 0.0 copy-start.3
  409.6 0.0 copy-start.2
  409.6 0.8 pad_maximum_fusion.2
  410.4 0.0 copy-done.5
  410.4 0.8 convert_element_type.41
  411.2 0.0 copy-done.4
  411.2 0.8 convert_element_type.46
  412.1 0.0 copy-done.3
  412.1 0.0 copy-start.1
  412.1 0.8 bitcast_convert_fusion
  412.9 0.0 copy-done.2
  412.9 1.3 convert_element_type.47
  414.2 0.0 copy-done.1
  414.2 0.0 copy-start
  414.2 1.3 convert_element_type.48
  415.5 0.0 copy-done
  415.5 1.2 convert_element_type.49
  (9 shorter events, 0.1 us)
Async XLA Ops:
  405.4 1.3 copy-start.6
  406.7 3.7 copy-start.5
  408.5 2.8 copy-start.4
  409.6 2.5 copy-start.3
  409.6 3.4 copy-start.2
  412.1 2.2 copy-start.1
  414.2 1.3 copy-start

commit v2 on v1

--- a/solution.py
+++ b/solution.py
@@ -3,6 +3,7 @@
 
 import jax
 import jax.numpy as jnp
+import numpy as np
 from jax import lax
 from jax.experimental import pallas as pl
 from jax.experimental.pallas import tpu as pltpu
@@ -402,7 +403,8 @@
 MESH = pl.DeviceIdType.MESH
 HBM = pl.BlockSpec(memory_space=pltpu.HBM)
 VM = pl.BlockSpec(memory_space=pltpu.VMEM)
-SLOTS = 256
+SLOTS = 368
+LOCAL_SLOTS = 18
 NT = (((1,), (1,)), ((), ()))
 TN = (((0,), (0,)), ((), ()))
 BF = jnp.bfloat16
@@ -433,9 +435,13 @@
     def shard(self, step):
         return lax.rem(self.c + step + self.C, self.C)
 
+    def slots(self, count):
+        self.used += count
+        assert self.used <= SLOTS
+        return self.used - count
+
     def slot(self):
-        self.used += 1
-        return self.used - 1
+        return self.slots(1)
 
     def remote(self, src, dst, slot, to):
         return pltpu.make_async_remote_copy(
@@ -445,6 +451,7 @@
 
     def local(self, src, dst):
         self.used_local += 1
+        assert self.used_local <= LOCAL_SLOTS
         return pltpu.make_async_copy(src, dst, self.loc.at[self.used_local - 1])
 
     def meet(self, devices):
@@ -466,7 +473,7 @@
         live = [p for p in live if next(p, 0) != 0]
 
 
-def gather_rows(net, src, dst, half):
+def gather_rows(net, src, dst, half, done=None):
     C, c, k, y = net.C, net.c, net.k, net.y
     H = dst.shape[-1] // 2
     mine = pl.ds(pl.multiple_of(y * H, 128), H)
@@ -477,6 +484,7 @@
     core, over_y = net.core(), net.over_y()
     keep = net.local(src, dst.at[k, c, :, own_cols])
     keep.start()
+    done = done or (lambda kk, q: None)
     hops = [(d, s) for s in range(1, C) for d in (0, 1)]
     zslot = {h: net.slot() for h in hops}
     yslot = {h: net.slot() for h in hops}
@@ -532,9 +540,13 @@
             piece = dst.at[k, q, :, other]
             net.remote(piece, piece, yslot[d, s], over_y).wait_recv()
             net.remote(piece, piece, bslot[d, s], core).start()
+            done(k, q)
         yield 1
+    keep.wait()
+    done(k, c)
     to_core_in = net.remote(src, dst.at[1 - k, c, :, own_cols], own_core, core)
     to_core_in.wait_recv()
+    done(1 - k, c)
     to_core_in.wait_send()
     if half:
         piece = dst.at[1 - k, c, :, other]
@@ -548,6 +560,7 @@
             a, b = dst.at[1 - k, q, :, mine], dst.at[1 - k, q, :, other]
             net.remote(a, a, aslot[d, s], core).wait()
             net.remote(b, b, bslot[d, s], core).wait()
+            done(1 - k, q)
             net.remote(a, a, yslot[d, s], over_y).wait_send()
 
         sent = jnp.logical_and(no_right if d == 0 else no_left, chunk(d, s - 1)[1])
@@ -556,7 +569,6 @@
         def _(d=d, s=s):
             piece = dst.at[k, c, :, mine]
             z_send(d, s, piece, c).wait_send()
-    keep.wait()
     yield 1
 
 
@@ -611,68 +623,150 @@
             keep.wait()
 
 
-def reduce_scratch(C, rows, width, tiles):
+class Columns:
+    def __init__(self, ref, first, width):
+        self.ref, self.first, self.width = ref, first, width
+        self.at = self
+
+    def lanes(self, j):
+        return pl.ds(pl.multiple_of((self.first + j) * self.width, 128), self.width)
+
+    def __getitem__(self, j):
+        return Slot(self.ref, self.lanes(j))
+
+    def __setitem__(self, j, value):
+        self.ref[:, :, self.lanes(j)] = value
+
+
+def Slot(ref, lanes):
+    return ref.at[:, :, lanes]
+
+
+def reduce_scratch(C, rows, width, tiles, wire):
     w = width // tiles
+    n = tiles // 2
     return [
-        pltpu.VMEM((tiles // 2, C, rows, w), BF),
-        pltpu.VMEM((tiles, C, rows, w), BF),
-        pltpu.VMEM((tiles // 2, C, rows, w), BF),
-        pltpu.VMEM((tiles // 2, C, rows, w), BF),
-        pltpu.VMEM((tiles // 2, C, rows, w), F32),
-        pltpu.VMEM((tiles // 2, C - 1, rows, w), BF),
-        pltpu.VMEM((tiles // 2, C - 1, rows, w), BF),
+        pltpu.VMEM((2, C, rows, w), wire),
+        pltpu.VMEM((tiles, C, rows, w), wire),
+        pltpu.VMEM((n, C, rows, w), BF),
+        pltpu.VMEM((n, C, rows, w), BF),
+        pltpu.VMEM((n, C, rows, w), F32),
+        pltpu.VMEM((n, C - 1, rows, w), BF),
+        pltpu.VMEM((n, C - 1, rows, w), BF),
+        pltpu.VMEM((n, rows, w), BF),
     ]
 
 
 def reduce_rows(net, product, scratch, out):
-    osend, orecv, ysend, yrecv, sums, zsend, zrecv = scratch
-    tiles, C, rows, w = orecv.shape
-    n = tiles // 2
-    k, y = net.k, net.y
+    osend, orecv, ysend, yrecv, sums, zsend, zrecv, joined = scratch
+    n, C, rows, w = zsend.shape
+    tiles, C = 2 * n, C + 1
+    c, k, y = net.c, net.k, net.y
     core, over_y = net.core(), net.over_y()
-    column = [(1 - y) * n + j for j in range(n)] + [y * n + j for j in range(n)]
-    copies = []
-    for j in range(tiles):
-        if j >= n:
-            copies[j - n].wait_send()
-        osend[j % n] = product(1 - k, column[j]).astype(BF).reshape(C, rows, w)
-        cp = net.remote(osend.at[j % n], orecv.at[j], net.slot(), core)
-        cp.start()
-        copies.append(cp)
-        yield 1
-    ycopies = []
+    depth = osend.shape[0]
+    cslot, yslot, jslot, zslot = net.slots(tiles), net.slots(n), net.slots(n), net.slots(n * (C - 1))
+
+    def to_core(j):
+        return net.remote(osend.at[j % depth], orecv.at[j], cslot + j, core)
+
+    def to_y(j):
+        return net.remote(ysend.at[j], yrecv.at[j], yslot + j, over_y)
+
+    def column(j):
+        return (j // n + 1 + y) % 2 * n + j % n
+
+    def step(j, _):
+        @pl.when(j < tiles)
+        def _():
+            @pl.when(j >= depth)
+            def _():
+                to_core(j - depth).wait_send()
+
+            osend[j % depth] = product(1 - k, column(j)).astype(osend.dtype).reshape(C, rows, w)
+            to_core(j).start()
+
+        @pl.when(j > 0)
+        def _():
+            i = j - 1
+            own = product(k, column(i)).reshape(C, rows, w)
+            to_core(i).wait_recv()
+            own = own + orecv.at[i][...].astype(F32)
+
+            @pl.when(i < n)
+            def _():
+                ysend[i % n] = own.astype(BF)
+                to_y(i % n).start()
+
+            @pl.when(i >= n)
+            def _():
+                sums[i % n] = own
+
+        return 0
+
+    lax.fori_loop(0, tiles + 1, step, 0)
+    yield 1
+    low, high = c == 0, c == C - 1
+    inner = jnp.logical_and(c > 0, c < C - 1)
+    beside = net.at(c=jnp.where(low, 1, C - 2))
+
+    def z(j, dc):
+        return net.remote(zsend.at[j, dc - 1], zrecv.at[j, dc - 1], zslot + j * (C - 1) + dc - 1, net.at(c=net.shard(dc)))
+
+    def join(j, dc):
+        return net.remote(zsend.at[j, dc - 1], joined.at[j], jslot + j, beside)
+
+    def through(j):
+        zsend[j, 1] = sums[j, net.shard(2)].astype(BF)
+
+        @pl.when(inner)
+        def _():
+            join(j, 2).wait_recv()
+            zsend[j, 1] = (sums[j, net.shard(2)] + joined[j].astype(F32)).astype(BF)
+
+        z(j, 2).start()
+
+    ends = ((1, high), (C - 1, low))
     for j in range(n):
-        own = product(k, column[j]).reshape(C, rows, w)
-        copies[j].wait_recv()
-        ysend[j] = (own + orecv[j].astype(F32)).astype(BF)
-        cp = net.remote(ysend.at[j], yrecv.at[j], net.slot(), over_y)
-        cp.start()
-        ycopies.append(cp)
-        yield 1
-    zcopies = []
-    for j in range(n):
-        own = product(k, column[n + j]).reshape(C, rows, w)
-        copies[n + j].wait_recv()
-        own = own + orecv[n + j].astype(F32)
-        sums[j] = own
-        ycopies[j].wait_recv()
-        sums[j] = sums[j] + yrecv[j].astype(F32)
-        for dc in range(1, C):
-            to = net.shard(dc)
-            zsend[j, dc - 1] = sums[j, to].astype(BF)
-            cp = net.remote(zsend.at[j, dc - 1], zrecv.at[j, dc - 1], net.slot(), net.at(c=to))
-            cp.start()
-            zcopies.append(cp)
+        to_y(j).wait_recv()
+        sums[j] = sums[j] + yrecv.at[j][...].astype(F32)
+        for dc, far in ends:
+            zsend[j, dc - 1] = sums[j, net.shard(dc)].astype(BF)
+
+            @pl.when(far)
+            def _(dc=dc):
+                join(j, dc).start()
+
+            @pl.when(jnp.logical_not(far))
+            def _(dc=dc):
+                z(j, dc).start()
+
+        if j:
+            through(j - 1)
+        if j == n - 1:
+            through(j)
         yield 1
     for j in range(n):
-        total = sums[j, net.c]
-        for dc in range(1, C):
-            zcopies[j * (C - 1) + dc - 1].wait_recv()
-            total = total + zrecv[j, dc - 1].astype(F32)
-        out[j] = total
+        z(j, 2).wait_recv()
+        out[j] = sums[j, c] + zrecv[j, 1].astype(F32)
+        for dc, absent in ((1, low), (C - 1, high)):
+            @pl.when(jnp.logical_not(absent))
+            def _(dc=dc):
+                z(j, dc).wait_recv()
+                out[j] = out[j] + zrecv[j, dc - 1].astype(F32)
         yield 1
-    for cp in copies[n:] + ycopies + zcopies:
-        cp.wait_send()
+    for j in range(n):
+        if j < depth:
+            to_core(tiles - depth + j).wait_send()
+        to_y(j).wait_send()
+        z(j, 2).wait_send()
+        for dc, far in ends:
+            @pl.when(far)
+            def _(dc=dc):
+                join(j, dc).wait_send()
+
+            @pl.when(jnp.logical_not(far))
+            def _(dc=dc):
+                z(j, dc).wait_send()
     yield 1
 
 
@@ -707,11 +801,12 @@
             return
 
 
-def front_kernel(C, tiles, head, scale, tile, x_ref, g_ref, cot, qp, kp, cosine, sine, wq, wk, wv, wo, wg, wu, wd,
-                 xg_out, ghg, wqkv, wod, wdd, gains, raw, q_out, kv, kvp, o_out, lse, act, h_out, gh_out, part_out,
-                 g_out, u_out, d_out, zgu, zd,
-                 xn, xg, ht, ct, wgu, m_s, l_s, acc, red, rs, hn, gb, s_out, s_in, s_out2, s_in2, ggu, ggu_t, act_t, from_x, to_x,
+def layer_kernel(C, tiles, head, scale, tile, few, x_ref, a_gain, m_gain, few_gains, cot, freq, pair, wq, wk, wv, wo, wg, wu, wd,
+                 xg_out, g_out, u_out, d_out, blk, ig, sums_out, q_grad, kv_grad, o_grad,
+                 g_ref, gains, h_out, gh_out, zgu, zd, mine, act, wdd, xg, ht, ct, wgu, m_s, l_s, acc, red, rs, hn, gb, stats,
+                 ggu, ggu_t, act_t, from_x, delta, own, peer, cin, xin, xq, zq, xo, zo, vec, vin, vx, vz, red_x, rs_x,
                  send, recv, loc):
+    qp, kp, cosine, sine, wqkv, wod, raw, q_out, kv, kvp, o_out, lse = mine
     net = Net(C, send, recv, loc)
     c, x, y, k = net.c, net.x, net.y, net.k
     B, unit = wg.shape[0], wdd.shape[0]
@@ -724,13 +819,16 @@
     mates = [net.at(c=net.shard(dc), x=(x + dx) % 2, k=(k + dk) % 2) for dc, dx, dk in plane]
     net.meet(mates + [net.over_y()])
     me = c * 4 + 2 * x + k
+    g_ref[...] = jnp.concatenate(
+        [a_gain[...].astype(F32), m_gain[...].astype(F32), pltpu.roll(few_gains[...], me * few, 1)[0:2],
+         jnp.zeros((12, B), F32)], axis=0).astype(BF)
     sent = []
     for to in mates:
         cp = net.remote(g_ref, gains.at[me], net.slot(), to)
         cp.start()
         sent.append(cp)
-    own = net.local(g_ref, gains.at[me])
-    own.start()
+    own_gains = net.local(g_ref, gains.at[me])
+    own_gains.start()
     full = slice(None)
     lanes = lambda n, m: pl.ds(pl.multiple_of(n * m, 128), m)
     rows = lambda b: pl.ds(pl.multiple_of(b * B, B), B)
@@ -750,19 +848,36 @@
            lambda b: wdd.at[:, lanes(b, B)])
     h_qkv, h_o, h_mlp = Hand(net, [g_qkv]), Hand(net, [g_o]), Hand(net, [g_gu, g_d])
     every = 2 * C
-    h_qkv.post(4)
-    own.wait()
+
+    def normalise(kk, q):
+        value = ht[kk, q].astype(F32)
+        hat = value * lax.rsqrt(jnp.mean(value * value, axis=-1, keepdims=True) + EPS)
+        for b in range(blocks):
+            t = pl.ds(b * B, B)
+            xg[kk, q, :, t] = (hat[:, b * B:(b + 1) * B] * gains[b].astype(F32)[0:1]).astype(BF)
+
+    rows_x = gather_rows(net, x_ref, ht, False, normalise)
+    next(rows_x)
+    h_qkv.post(2)
+    for kk in range(2):
+        for q in range(C):
+            base = jnp.where(x == 0, pair[q], 2 * C - 1 - pair[q]) * (2 * R) + kk * R
+            r = pl.ds((kk * C + q) * R, R)
+            spot = lax.broadcasted_iota(jnp.int32, (R, 128), 0) + base
+            qp[r] = spot
+            kp[:, r] = lax.broadcasted_iota(jnp.int32, (8, R), 1) + base
+            angle = spot.astype(F32) * freq[0:1]
+            sign = jnp.where(lax.broadcasted_iota(jnp.int32, (R, 128), 1) < head // 2, -1.0, 1.0)
+            cosine[r] = jnp.cos(angle)
+            sine[r] = jnp.sin(angle) * sign
+
+    for _ in range(C - 1):
+        steps_of(rows_x, 2)
+        h_qkv.post(2)
+        h_qkv.relay(2)
+    own_gains.wait()
     for cp in sent:
         cp.wait()
-    value = x_ref[...].astype(F32)
-    hat = value * lax.rsqrt(jnp.mean(value * value, axis=-1, keepdims=True) + EPS)
-    xn[...] = times_gain(hat, [gains[b].astype(F32)[0:1] for b in range(blocks)]).astype(BF)
-    rows_x = gather_rows(net, xn, xg, False)
-    next(rows_x)
-    h_qkv.post(every - 4)
-    for _ in range(C - 1):
-        steps_of(rows_x, 2)
-        h_qkv.relay(2)
     h_qkv.relay(1)
     run(rows_x)
     h_qkv.finish()
@@ -836,7 +951,7 @@
                        preferred_element_type=F32)
 
     reduce = reduce_rows(net, product, red, rs)
-    steps_of(reduce, tiles + tiles // 2)
+    next(reduce)
     h_mlp.relay(2)
     for _ in range(tiles // 2):
         steps_of(reduce, 1)
@@ -846,7 +961,7 @@
     h_mlp.relay(every - 3 - tiles // 2)
     run(reduce)
     half = half_of(x_ref, y, H).astype(F32) + jnp.concatenate([rs[j] for j in range(tiles // 2)], axis=1)
-    total = swap_sums(net, jnp.sum(half * half, axis=-1, keepdims=True), s_out, s_in)
+    total = swap_sums(net, jnp.sum(half * half, axis=-1, keepdims=True), stats.at[0], stats.at[1])
     hs = lax.rsqrt(total / D + EPS)
     h_out[...] = half
     hn[...] = times_gain(half * hs, gain_half(gains, y, 1, blocks // 2)).astype(BF)
@@ -890,20 +1005,27 @@
 
     swaps = []
 
+    def to_x(q):
+        if q < C - 1:
+            return wgu.at[pl.ds(0, 2 * unit), pl.ds(q * pair, pair)], wgu.at[pl.ds(2 * unit, unit), pl.ds(q * pair, pair)]
+        return wgu.at[pl.ds(3 * unit, 2 * unit), pl.ds(0, pair)], wgu.at[pl.ds(3 * unit, unit), pl.ds(pair, pair)]
+
     def send_partial(q):
         def out(a, b, v):
-            to_x[q, a:b] = v.astype(BF)
+            to_x(q)[a // (2 * unit)][...] = v.astype(BF)
 
         weight_grads(net.shard(q + 1) * 2 + 1 - x, out)
-        cp = net.remote(to_x.at[q], from_x.at[q], net.slot(), net.over_x())
-        cp.start()
-        swaps.append(cp)
+        pieces = pl.ds(0, 2 * unit), pl.ds(2 * unit, unit)
+        swaps.append([net.remote(a, from_x.at[q, r], net.slot(), net.over_x()) for a, r in zip(to_x(q), pieces)])
+        for cp in swaps[q]:
+            cp.start()
 
     place = lambda a, b, m: pl.ds(pl.multiple_of((2 * a + b) * m, 128), m)
 
     def add_partial(q):
         dc = (q + 1) % C
-        swaps[q].wait_recv()
+        for cp in swaps[q]:
+            cp.wait_recv()
 
         def out(a, b, v):
             v = v + from_x[q, a:b].astype(F32)
@@ -917,174 +1039,85 @@
 
         weight_grads(net.shard(dc) * 2 + x, out)
 
+    keep.wait()
     hand_out = Deal(net, swiglu_groups(g_out, u_out, d_out, zgu, zd, unit))
     reduce = reduce_rows(net, normed, red, rs)
-    steps_of(reduce, tiles + tiles // 2)
+    next(reduce)
     for q in range(C):
         send_partial(q)
         steps_of(reduce, tiles // 2 // C)
-    add_partial(0)
-    hand_out.post(2)
     run(reduce)
     g = jnp.concatenate([rs[j] for j in range(tiles // 2)], axis=1)
     hat = half * hs
     col = jnp.sum(g * hat, axis=0, keepdims=True)
-    for i in range(part_out.shape[0]):
-        n = part_out.shape[1]
-        part_out[i:i + 1] = col[:, i * n:(i + 1) * n]
+    n = vec.shape[2]
+    count = H // n
+    vec[0] = jnp.zeros(vec.shape[1:], F32)
+    for i in range(count):
+        vec[0, count + i:count + i + 1] = col[:, i * n:(i + 1) * n]
     m = times_gain(g, gain_half(gains, y, 1, blocks // 2))
-    mean = swap_sums(net, jnp.sum(m * hat, axis=-1, keepdims=True), s_out2, s_in2) / D
+    mean = swap_sums(net, jnp.sum(m * hat, axis=-1, keepdims=True), stats.at[2], stats.at[3]) / D
     gh = half_of(cot, y, H).astype(F32) + hs * (m - hat * mean)
     gh_out[...] = gh
     gb[...] = gh.astype(BF)
-    rows_g = gather_rows(net, gb, ghg, True)
+    rows_g = gather_rows(net, gb, xg, True)
     next(rows_g)
+    add_partial(0)
+    steps_of(rows_g, 2)
     add_partial(1)
+    steps_of(rows_g, 4)
+    add_partial(2)
     run(rows_g)
-    add_partial(2)
-    add_partial(3)
-    hand_out.finish()
-    for cp in swaps:
-        cp.wait_send()
-    keep.wait()
-
-
-def swiglu_groups(g_out, u_out, d_out, zgu, zd, unit):
-    full = slice(None)
-    place = lambda a, b: pl.ds(pl.multiple_of((2 * a + b) * unit, 128), unit)
-    return [
-        (None, None, None, zgu,
-         [((full, pl.ds(0, unit)), lambda a, b: g_out.at[:, place(a, b)]),
-          ((full, pl.ds(unit, unit)), lambda a, b: u_out.at[:, place(a, b)])], None, False),
-        (None, None, None, zd, [((full, full), lambda a, b: d_out.at[place(a, b), :])], None, False),
-    ]
-
-
-class Deal:
-    def __init__(self, net, groups):
-        self.net, self.groups = net, groups
-        self.order = [(dc, dk) for dc in range(1, net.C) for dk in range(2)] + [(0, 1), (0, 0)]
-        self.xs, self.zs = {}, []
-        self.added = self.posted = 0
-
-    def start(self):
-        net = self.net
-        for s in self.order:
-            b = net.shard(s[0]) * 4 + 2 * (1 - net.x) + (net.k + s[1]) % 2
-            for g, (partial, place, from_x, *_) in enumerate(self.groups):
-                cp = net.remote(partial.at[place(b)], from_x.at[2 * s[0] + s[1]], net.slot(), net.over_x())
-                cp.start()
-                self.xs[g, s] = cp
-
-    def add(self, count):
-        net = self.net
-        for s in self.order[self.added:self.added + count]:
-            i = 2 * s[0] + s[1]
-            b = net.shard(s[0]) * 4 + 2 * net.x + (net.k + s[1]) % 2
-            for g, (partial, place, from_x, sums, puts, keep, flip) in enumerate(self.groups):
-                self.xs[g, s].wait_recv()
-                total = partial[place(b)].astype(F32) + from_x[i].astype(F32)
-                if flip:
-                    total = total.T
-                if s == (0, 0) and keep is not None:
-                    keep(total)
-                else:
-                    sums[i] = total.astype(BF)
-        self.added += count
-
-    def post(self, count):
-        net = self.net
-        for s in self.order[self.posted:min(self.posted + count, len(self.order) - 1)]:
-            i = 2 * s[0] + s[1]
-            to = net.at(c=net.shard(s[0]), k=(net.k + s[1]) % 2)
-            for partial, place, from_x, sums, puts, keep, flip in self.groups:
-                slot = net.slot()
-                for take, put in puts:
-                    net.remote(sums.at[(i,) + take], put(net.c, net.k), slot, to).start()
-                self.zs.append((sums, i, slot))
-        self.posted += count
-
-    def both(self, count):
-        for _ in range(count):
-            self.add(1)
-            self.post(1)
-
-    def finish(self):
-        for sums, i, slot in self.zs:
-            self.net.remote(sums.at[i], sums.at[i], slot, self.net.over_x()).wait()
-        for cp in self.xs.values():
-            cp.wait_send()
-
-
-def back_kernel(C, tiles, head, scale, tile, q_ref, kv, kvp, o_ref, lse, qp, kp, cosine, sine, raw, wqkv, wod, gains,
-                x_ref, gh_ref, h_ref, parts, act, wdd, zgu, zd, g_in, u_in, d_in, ghg, xg,
-                blk, ig, sums_out, g_out, u_out, d_out, q_out, kv_out, o_out,
-                gt, xt, do, delta, dq, own, peer, kvg, cin, xs, xin, gqk, dqk, dow, xq, zq, xo, zo, vec, vin, vx, vz,
-                s_out, s_in, red_d, rs_d, red, rs, send, recv, loc):
-    net = Net(C, send, recv, loc)
-    c, x, y, k = net.c, net.x, net.y, net.k
-    T = q_ref.shape[0]
-    R, D = x_ref.shape
-    H = D // 2
-    w = D // tiles
-    blocks = gains.shape[0]
-    load_g = net.local(ghg, gt)
-    load_x = net.local(xg, xt)
-    load_g.start()
-    load_x.start()
-    unit, B = wdd.shape[0], u_out.shape[0]
-    place = lambda a, b, m: pl.ds(pl.multiple_of((2 * a + b) * m, 128), m)
-    g_out[...], u_out[...], d_out[...] = g_in[...], u_in[...], d_in[...]
-    g_out[:, place(c, k, unit)] = zgu[0, :, 0:unit]
-    u_out[:, place(c, k, unit)] = zgu[0, :, unit:2 * unit]
-    d_out[place(c, k, unit), :] = zd[0]
-    net.meet(net.group() + [net.over_x(), net.over_y()])
-    full = slice(None)
-    lanes = lambda n, m: pl.ds(pl.multiple_of(n * m, 128), m)
-    deal_u = Deal(net, swiglu_groups(g_out, u_out, d_out, zgu, zd, unit))
-    deal_u.posted = 2
-    deal_u.post(2 * C)
-    steps = T // tile
-    half = T // 2
+    hand_out.post(6)
 
     def rows_of(i):
         return pl.ds(pl.multiple_of(i * tile, tile), tile)
-
-    load_g.wait()
 
     def grad_o(i, _):
         r = rows_of(i)
         per = tile // R
-        g = lax.dot_general(gt[i // (steps // 2), pl.ds((i % (steps // 2)) * per, per)].reshape(tile, D), wod[...], NT,
+        g = lax.dot_general(xg[i // (steps // 2), pl.ds((i % (steps // 2)) * per, per)].reshape(tile, D), wod[...], NT,
                             preferred_element_type=F32).astype(BF)
-        do[r] = g
-        d = jnp.sum(g.astype(F32) * o_ref[r].astype(F32), axis=-1, keepdims=True)
+        ggu[i // (steps // 2), pl.ds(pl.multiple_of(i % (steps // 2) * tile, tile), tile), pl.ds(2 * head, head)] = g
+        d = jnp.sum(g.astype(F32) * o_out[r].astype(F32), axis=-1, keepdims=True)
         delta[:, r] = jnp.broadcast_to(d, (tile, 128)).T[0:8]
         return 0
 
     lax.fori_loop(0, steps, grad_o, 0)
-    dq[...] = jnp.zeros_like(dq)
+    add_partial(C - 1)
+    hand_out.post(2)
+    keeps = [net.local(zgu.at[0, :, pl.ds(0, unit)], g_out.at[:, place(c, k, unit)]),
+             net.local(zgu.at[0, :, pl.ds(unit, unit)], u_out.at[:, place(c, k, unit)]),
+             net.local(zd.at[0], d_out.at[place(c, k, unit), :])]
+    load_x = net.local(xg_out, ct)
+    for cp in keeps + [load_x]:
+        cp.start()
+    for copies in swaps:
+        for cp in copies:
+            cp.wait_send()
+    acc[...] = jnp.zeros_like(acc)
     own[...] = jnp.zeros_like(own)
 
     def sweep(keys, grads, masked):
         def step(i, _):
             r = rows_of(i)
-            q, g = q_ref[r], do[r]
+            q = q_out[r]
+            g = ggu[i // (steps // 2), pl.ds(pl.multiple_of(i % (steps // 2) * tile, tile), tile), pl.ds(2 * head, head)]
             s = lax.dot_general(keys[:, :head], q, NT, preferred_element_type=F32) * scale
             p = jnp.exp(s - lse[0:1, r])
             if masked:
-                p = jnp.where(kp[:, 0:1] <= qp[0:1, r], p, 0.0)
+                p = jnp.where(qp[:, 0:1] <= kp[0:1, r], p, 0.0)
             grads[1] += jnp.dot(p.astype(BF), g, preferred_element_type=F32)
             dp = lax.dot_general(keys[:, head:], g, NT, preferred_element_type=F32)
             ds = (p * (dp - delta[0:1, r])).astype(BF)
             grads[0] += jnp.dot(ds, q, preferred_element_type=F32)
-            dq[r] += lax.dot_general(ds, keys[:, :head], TN, preferred_element_type=F32)
+            acc[r] += lax.dot_general(ds, keys[:, :head], TN, preferred_element_type=F32)
             return 0
 
         lax.fori_loop(0, steps, step, 0)
 
     one = net.remote(peer.at[1 - k], cin.at[0], net.slot(), net.core())
-    two = net.remote(xs, xin, net.slot(), net.over_x())
+    two = net.remote(l_s, xin, net.slot(), net.over_x())
     three = net.remote(own.at[1 - k], cin.at[1], net.slot(), net.core())
 
     @pl.when(x == 1)
@@ -1093,7 +1126,7 @@
         sweep(kvp, peer, False)
         one.start()
         one.wait()
-        xs[...] = peer[k] + cin[0]
+        l_s[...] = peer[k] + cin[0]
         two.start()
 
     sweep(kv, own, True)
@@ -1102,13 +1135,8 @@
     def down(kk, t):
         return jnp.dot(act[kk], wdd[:, lanes(t, w)], preferred_element_type=F32)
 
-    reduce_d = reduce_rows(net, down, red_d, rs_d)
-    steps_of(reduce_d, tiles + tiles // 2)
-    gain_sum = jnp.sum(gains[...].astype(F32), axis=0)
-    qg, kg = gain_sum[2:3], gain_sum[3:4]
-    n = vec.shape[2]
-    count = H // n
-    vec[0] = parts[...]
+    reduce_d = reduce_rows(net, down, red, rs)
+    next(reduce_d)
 
     def back_norm(grad, value, gain, r):
         rotated = grad * cosine[r] - pltpu.roll(grad, head // 2, 1) * sine[r]
@@ -1120,14 +1148,23 @@
 
     def finish_q(i, total):
         r = rows_of(i)
-        g, col = back_norm(dq[r] * scale, raw[r, 0:head], qg, r)
-        gqk[r, 0:head] = g.astype(BF)
+        g, col = back_norm(acc[r] * scale, raw[r, 0:head], qg, r)
+        ggu[i // (steps // 2), pl.ds(pl.multiple_of(i % (steps // 2) * tile, tile), tile), pl.ds(0, head)] = g.astype(BF)
         return total + col
 
     vec[0, 2 * count:2 * count + 1] = lax.fori_loop(0, steps, finish_q, jnp.zeros((1, head), F32))
-    dow[...] = lax.dot_general(o_ref[...], gt[...].reshape(T, D), TN, preferred_element_type=F32).astype(BF)
+    def keep_o(v):
+        o_grad[place(c, k, head), :] = v.astype(BF)
+
+    deal_o = Deal(net, [
+        (from_x, lambda b: (2, pl.ds(pl.multiple_of(b // 2 * head, head), head), lanes(b % 2, B)), xo, zo,
+         [((full, full), lambda a, b: o_grad.at[place(a, b, head), :])], keep_o, False),
+    ])
+    for i in range(tiles):
+        from_x[2, pl.ds(i * head, head), :] = lax.dot_general(
+            o_out[...], xg[:, :, :, pl.ds(i * w, w)].reshape(T, w), TN, preferred_element_type=F32).astype(BF)
     three.wait()
-    kvg[...] = own[k] + cin[1]
+    m_s[...] = own[k] + cin[1]
 
     @pl.when(x == 1)
     def _():
@@ -1136,64 +1173,65 @@
     @pl.when(x == 0)
     def _():
         two.wait_recv()
-        kvg[...] = kvg[...] + xin[...]
+        m_s[...] = m_s[...] + xin[...]
 
     def finish_kv(i, total):
         r = rows_of(i)
-        v = kvg[r]
+        v = m_s[r]
         g, col = back_norm(v * scale, raw[r, head:2 * head], kg, r)
-        gqk[r, head:2 * head] = jnp.where(k == 0, g, v).astype(BF)
+        ggu[i // (steps // 2), pl.ds(pl.multiple_of(i % (steps // 2) * tile, tile), tile), pl.ds(head, head)] = jnp.where(k == 0, g, v).astype(BF)
         return total + jnp.where(k == 0, col, 0.0)
 
+    deal_o.start()
     vec[0, 2 * count + 1:2 * count + 2] = lax.fori_loop(0, steps, finish_kv, jnp.zeros((1, head), F32))
 
     def product(kk, t):
-        r = pl.ds(pl.multiple_of(kk * half, half), half)
-        a = lax.dot_general(gqk[r, 0:head], wqkv[lanes(t, w), 0:head], NT, preferred_element_type=F32)
-        return a + lax.dot_general(gqk[r, head:2 * head], wqkv[lanes(t, w), lanes(1 + k, head)], NT,
+        a = lax.dot_general(ggu[kk, :, 0:head], wqkv[lanes(t, w), 0:head], NT, preferred_element_type=F32)
+        return a + lax.dot_general(ggu[kk, :, head:2 * head], wqkv[lanes(t, w), lanes(1 + k, head)], NT,
                                    preferred_element_type=F32)
 
     def keep_q(v):
-        q_out[:, place(c, k, head)] = v[:, :head].astype(BF)
-        kv_out[k, :, lanes(c, head)] = v[:, head:].astype(BF)
-
-    def keep_o(v):
-        o_out[place(c, k, head), :] = v.astype(BF)
+        q_grad[:, place(c, k, head)] = v[:, :head].astype(BF)
+        kv_grad[k, :, lanes(c, head)] = v[:, head:].astype(BF)
 
     deal_q = Deal(net, [
-        (dqk, lambda b: (full, lanes(b, B)), xq, zq,
-         [((full, pl.ds(0, head)), lambda a, b: q_out.at[:, place(a, b, head)]),
-          ((full, pl.ds(head, head)), lambda a, b: kv_out.at[b, :, lanes(a, head)])], keep_q, True),
-        (dow, lambda b: (full, lanes(b, B)), xo, zo,
-         [((full, full), lambda a, b: o_out.at[place(a, b, head), :])], keep_o, False),
+        (from_x, lambda b: (b // 8, pl.ds(pl.multiple_of(b // 2 % 4 * (2 * head), 2 * head), 2 * head), lanes(b % 2, B)), xq, zq,
+         [((full, pl.ds(0, head)), lambda a, b: q_grad.at[:, place(a, b, head)]),
+          ((full, pl.ds(head, head)), lambda a, b: kv_grad.at[b, :, lanes(a, head)])], keep_q, True),
     ])
-    reduce = reduce_rows(net, product, red, rs)
-    steps_of(reduce, tiles + tiles // 2)
+    steps_of(reduce_d, 1)
+    reduce = reduce_rows(net, product, red_x, rs_x)
     load_x.wait()
+    next(reduce)
     for i in range(tiles):
         t = pl.ds(i * w, w)
-        dqk[:, t] = lax.dot_general(gqk[...], xt[:, :, :, t].reshape(T, w), TN, preferred_element_type=F32).astype(BF)
+        from_x[i // 4, pl.ds(i % 4 * 2 * head, 2 * head), :] = lax.dot_general(
+            ggu[:, :, 0:2 * head].reshape(T, 2 * head), ct[:, :, :, t].reshape(T, w), TN,
+            preferred_element_type=F32).astype(BF)
     deal_q.start()
-    steps_of(reduce_d, tiles // 2)
-    steps_of(reduce, tiles // 2)
+    steps_of(reduce, 1)
+    for _ in range(tiles // 2 - 1):
+        steps_of(reduce_d, 1)
+        steps_of(reduce, 1)
+    deal_o.both(2 * C)
     deal_q.both(2 * C)
     run(reduce_d)
-    blk[y] = (h_ref[...] + jnp.concatenate([rs_d[j] for j in range(tiles // 2)], axis=1)).astype(BF)
+    blk[y] = (h_out[...] + jnp.concatenate([rs[j] for j in range(tiles // 2)], axis=1)).astype(BF)
     swap_b = net.remote(blk.at[y], blk.at[y], net.slot(), net.over_y())
     swap_b.start()
     run(reduce)
     value = x_ref[...].astype(F32)
     xscale = lax.rsqrt(jnp.mean(value * value, axis=-1, keepdims=True) + EPS)
     hat = half_of(x_ref, y, H).astype(F32) * xscale
-    g = jnp.concatenate([rs[j] for j in range(tiles // 2)], axis=1)
+    g = jnp.concatenate([rs_x[j] for j in range(tiles // 2)], axis=1)
     col = jnp.sum(g * hat, axis=0, keepdims=True)
     for i in range(count):
         vec[0, i:i + 1] = col[:, i * n:(i + 1) * n]
     first = net.remote(vec.at[0], vin, net.slot(), net.core())
     first.start()
     m = times_gain(g, gain_half(gains, y, 0, blocks // 2))
-    mean = swap_sums(net, jnp.sum(m * hat, axis=-1, keepdims=True), s_out, s_in) / D
-    ig[y] = (gh_ref[...] + xscale * (m - hat * mean)).astype(BF)
+    mean = swap_sums(net, jnp.sum(m * hat, axis=-1, keepdims=True), stats.at[4], stats.at[5]) / D
+    ig[y] = (gh_out[...] + xscale * (m - hat * mean)).astype(BF)
     swap = net.remote(ig.at[y], ig.at[y], net.slot(), net.over_y())
     swap.start()
     first.wait()
@@ -1215,21 +1253,113 @@
     sums_out[y] = total
     last = net.remote(sums_out.at[y], sums_out.at[y], net.slot(), net.over_y())
     last.start()
-    deal_u.finish()
+    hand_out.finish()
+    deal_o.finish()
     deal_q.finish()
     last.wait()
     swap.wait()
     swap_b.wait()
+    for cp in keeps:
+        cp.wait()
+
+
+def swiglu_groups(g_out, u_out, d_out, zgu, zd, unit):
+    full = slice(None)
+    place = lambda a, b: pl.ds(pl.multiple_of((2 * a + b) * unit, 128), unit)
+    return [
+        (None, None, None, zgu,
+         [((full, pl.ds(0, unit)), lambda a, b: g_out.at[:, place(a, b)]),
+          ((full, pl.ds(unit, unit)), lambda a, b: u_out.at[:, place(a, b)])], None, False),
+        (None, None, None, zd, [((full, full), lambda a, b: d_out.at[place(a, b), :])], None, False),
+    ]
+
+
+class Deal:
+    def __init__(self, net, groups):
+        self.net, self.groups = net, groups
+        self.order = [(dc, dk) for dc in range(1, net.C) for dk in range(2)] + [(0, 1), (0, 0)]
+        self.xs, self.zs = {}, []
+        self.added = self.posted = 0
+
+    def start(self):
+        net = self.net
+        for s in self.order:
+            b = net.shard(s[0]) * 4 + 2 * (1 - net.x) + (net.k + s[1]) % 2
+            for g, (partial, place, from_x, *_) in enumerate(self.groups):
+                cp = net.remote(partial.at[place(b)], from_x.at[2 * s[0] + s[1]], net.slot(), net.over_x())
+                cp.start()
+                self.xs[g, s] = cp
+
+    def add(self, count):
+        net = self.net
+        for s in self.order[self.added:self.added + count]:
+            i = 2 * s[0] + s[1]
+            b = net.shard(s[0]) * 4 + 2 * net.x + (net.k + s[1]) % 2
+            for g, (partial, place, from_x, sums, puts, keep, flip) in enumerate(self.groups):
+                self.xs[g, s].wait_recv()
+                total = partial[place(b)].astype(F32) + from_x[i].astype(F32)
+                if flip:
+                    total = total.T
+                if s == (0, 0) and keep is not None:
+                    keep(total)
+                else:
+                    sums[i] = total.astype(BF)
+        self.added += count
+
+    def post(self, count):
+        net = self.net
+        for s in self.order[self.posted:min(self.posted + count, len(self.order) - 1)]:
+            i = 2 * s[0] + s[1]
+            to = net.at(c=net.shard(s[0]), k=(net.k + s[1]) % 2)
+            for partial, place, from_x, sums, puts, keep, flip in self.groups:
+                slot = net.slot()
+                for take, put in puts:
+                    net.remote(sums.at[(i,) + take], put(net.c, net.k), slot, to).start()
+                self.zs.append((sums, i, slot))
+        self.posted += count
+
+    def both(self, count):
+        for _ in range(count):
+            self.add(1)
+            self.post(1)
+
+    def finish(self):
+        for sums, i, slot in self.zs:
+            self.net.remote(sums.at[i], sums.at[i], slot, self.net.over_x()).wait()
+        for cp in self.xs.values():
+            cp.wait_send()
+
+
+def finish_kernel(few, blk, ig, sums, g, u, d, q, kv, o, block_out, input_grad, a_gain, q_w, k_w, v_w, q_gain, k_gain,
+                  o_w, m_gain, g_w, u_w, d_w):
+    mine = lax.axis_index(CONTEXT) * 4 + lax.axis_index(FSDP)
+    H = blk.shape[2]
+    n = H // sums.shape[2]
+    for i in range(2):
+        block_out[:, i * H:(i + 1) * H] = blk[i]
+        input_grad[:, i * H:(i + 1) * H] = ig[i].astype(F32)
+    for out, value in ((q_w, q), (o_w, o), (g_w, g), (u_w, u), (d_w, d)):
+        out[...] = value[...].astype(F32)
+    k_w[...] = kv[0].astype(F32)
+    v_w[...] = kv[1].astype(F32)
+    half, row = mine // n, mine % n
+    a_gain[...] = sums[half, pl.ds(row, 1)]
+    m_gain[...] = sums[half, pl.ds(n + row, 1)]
+    lanes = sums.shape[2]
+    total = sums[0] + sums[1]
+    shift = lax.rem(lanes - mine * few, lanes)
+    q_gain[...] = pltpu.roll(total[2 * n:2 * n + 8], shift, 1)[0:1, 0:few]
+    k_gain[...] = pltpu.roll(total[2 * n:2 * n + 8], shift, 1)[1:2, 0:few]
 
 
 def call(kernel, name, cid, out_shape, in_specs, out_specs, scratch, *args):
     return pl.pallas_call(
         kernel, name=name, out_shape=out_shape, in_specs=in_specs, out_specs=out_specs,
         scratch_shapes=scratch + [
-            pltpu.SemaphoreType.DMA((SLOTS,)), pltpu.SemaphoreType.DMA((SLOTS,)), pltpu.SemaphoreType.DMA((32,)),
+            pltpu.SemaphoreType.DMA((SLOTS,)), pltpu.SemaphoreType.DMA((SLOTS,)), pltpu.SemaphoreType.DMA((LOCAL_SLOTS,)),
         ],
         compiler_params=pltpu.CompilerParams(
-            collective_id=cid, has_side_effects=True, vmem_limit_bytes=60 * 1024 * 1024
+            collective_id=cid, has_side_effects=True, vmem_limit_bytes=67043328
         ),
     )(*args)
 
@@ -1245,74 +1375,78 @@
     head = HEAD_SIZE
     unit = gate_weight.shape[1] // (2 * C)
     scale = 1.0 / math.sqrt(head)
-    half = head // 2
     S = jax.ShapeDtypeStruct
     k = lax.axis_index(FSDP) % 2
     x = lax.axis_index(FSDP) // 2
     TILES = 8
 
-    red = lambda: reduce_scratch(C, R, D, TILES)
+    red = lambda wire: reduce_scratch(C, R, D, TILES, wire)
     rs = lambda: pltpu.VMEM((TILES // 2, R, D // TILES), F32)
     stat = lambda: pltpu.VMEM((R, 128), F32)
     mine = lax.axis_index(CONTEXT) * 4 + lax.axis_index(FSDP)
-    spread = lambda v: lax.dynamic_update_slice_in_dim(jnp.zeros((head,), BF), v, mine * v.shape[0], 0)
-    packed = jnp.pad(jnp.stack([attn_gain, mlp_gain, spread(q_gain), spread(k_gain)]), ((0, 12), (0, 0)))
-    order = jnp.arange(T, dtype=jnp.int32)
-    ids = (order // R % C) * (4 * R) + x * (2 * R) + (order // (C * R)) * R + order % R
-    places = row_places(block_pair, ids, 2 * R)
-    cosine, sine = (t[:, 0, :] for t in rope_tables(places, head))
-    cosine = jnp.concatenate([cosine, cosine], axis=1)
-    sine = jnp.concatenate([-sine, sine], axis=1)
-    p_col = jnp.broadcast_to(places[:, None], (T, 128))
-    p_row = jnp.broadcast_to(places[None, :], (8, T))
+    rows_of = lambda v: v.reshape(1, -1)
+    freq = np.exp(np.arange(head // 2, dtype=np.float32) * np.float32(-2.0 * math.log(THETA) / head))
+    freq = np.broadcast_to(np.concatenate([freq, freq])[None, :], (8, head))
+    small = jnp.pad(jnp.stack([q_gain, k_gain]), ((0, 6), (0, head - q_gain.shape[0]))).astype(F32)
     vm = lambda *shape: pltpu.VMEM(shape, BF)
-    (xg, ghg, wqkv, wo, wd, gains, raw, q_rot, kv, kvp, attn_o, lse, act, h_half, gh_half, mlp_part, g_in, u_in, d_in,
-     zgu, zd) = call(
-        lambda *r: front_kernel(C, TILES, head, scale, 256, *r[:43], r[43:50], *r[50:]), "front", 1,
-        (S((2, C, R, D), BF), S((2, C, R, D), BF), S((D, 3 * head), BF), S((head, D), BF), S((unit, D), BF),
-         S((NB, 16, B), BF), S((T, 2 * head), F32), S((T, head), BF), S((T, 2 * head), BF), S((T, 2 * head), BF),
-         S((T, head), BF), S((8, T), F32), S((2, C * R, unit), BF), S((R, H), F32), S((R, H), F32),
-         S((H // 128, 128), F32), S((B, 2 * C * unit), BF), S((B, 2 * C * unit), BF), S((2 * C * unit, B), BF),
-         S((2 * C, B, 2 * unit), BF), S((2 * C, unit, B), BF)),
-        [VM] * 7 + [HBM] * 7, (HBM,) * 2 + (VM,) * 19,
-        [vm(R, D), vm(2, C, R, D), vm(2, C, R, D), vm(2, C, R, D), vm(D, 2 * unit), pltpu.VMEM((T, 128), F32),
-         pltpu.VMEM((T, 128), F32), pltpu.VMEM((T, head), F32)] + red()
-        + [rs(), vm(R, H), vm(R, H), stat(), stat(), stat(), stat(), vm(2, C * R, 2 * unit), vm(2 * unit, T),
-           vm(unit, T), vm(C, 3 * unit, 2 * B), vm(C, 3 * unit, 2 * B)],
-        layer_input, packed, cotangent, p_col, p_row, cosine, sine,
-        q_weight, key_projection, value_projection, o_weight, gate_weight, up_weight, down_weight,
-    )
-    n_rows = H // 128
-    parts = jnp.concatenate([jnp.zeros_like(mlp_part), mlp_part, jnp.zeros((8, 128), F32)], axis=0)
-    V = parts.shape
+    f32 = lambda *shape: pltpu.VMEM(shape, F32)
+    mine_s = [pltpu.VMEM((T, 128), jnp.int32), pltpu.VMEM((8, T), jnp.int32), f32(T, 128), f32(T, 128), vm(D, 3 * head),
+              vm(head, D), f32(T, 2 * head), vm(T, head), vm(T, 2 * head), vm(T, 2 * head), vm(T, head), f32(8, T)]
+    E = len(mine_s)
+    V = (2 * (H // 128) + 8, 128)
     wide = lambda: pltpu.VMEM((2, T, head), F32)
     one = lambda: pltpu.VMEM((T, head), F32)
-    blk, ig, sums, g_w, u_w, d_w, q_w, kv_w, o_w = call(
-        lambda *r: back_kernel(C, TILES, head, scale, 256, *r[:59], r[59:66], r[66], r[67:74], *r[74:]), "back", 3,
-        (S((2, R, H), BF), S((2, R, H), BF), S((2,) + V, F32), S((B, 2 * C * unit), BF), S((B, 2 * C * unit), BF),
-         S((2 * C * unit, B), BF), S((B, 2 * C * head), BF), S((2, B, C * head), BF), S((2 * C * head, B), BF)),
-        [VM] * 24 + [HBM] * 2, (VM,) * 9,
-        [pltpu.VMEM((2, C, R, D), BF), pltpu.VMEM((2, C, R, D), BF), pltpu.VMEM((T, head), BF), pltpu.VMEM((8, T), F32),
-         one(), wide(), wide(), one(), wide(), one(), one(), pltpu.VMEM((T, 2 * head), BF),
-         pltpu.VMEM((2 * head, D), BF), pltpu.VMEM((head, D), BF), pltpu.VMEM((2 * C, 2 * head, B), BF),
-         pltpu.VMEM((2 * C, B, 2 * head), BF), pltpu.VMEM((2 * C, head, B), BF), pltpu.VMEM((2 * C, head, B), BF),
-         pltpu.VMEM((2,) + V, F32), pltpu.VMEM(V, F32), pltpu.VMEM(V, F32), pltpu.VMEM((C,) + V, F32), stat(), stat()]
-        + red() + [rs()] + red() + [rs()],
-        q_rot, kv, kvp, attn_o, lse, p_row, p_col, cosine, sine, raw, wqkv, wo, gains, layer_input, gh_half, h_half,
-        parts, act, wd, zgu, zd, g_in, u_in, d_in, ghg, xg,
-    )
-    join = lambda v: jnp.concatenate([v[0], v[1]], axis=1)
-    both = sums[:, :n_rows].reshape(2 * n_rows, 128)
-    both_mlp = sums[:, n_rows:2 * n_rows].reshape(2 * n_rows, 128)
-    pick = lambda v: lax.dynamic_slice_in_dim(v.reshape(-1), mine * B, B)
+    narrow = red(BF)
+    inner = [narrow[0]] + narrow[4:]
+
+    def layer(*r):
+        a = 24 + 6
+        b = a + E
+        c = b + 9
+        d = c + 8
+        e = d + 8 + 13
+        osend, *rest = r[e:e + 5]
+        ht = r[b + 3]
+        views = (osend, Columns(ht.at[0], 0, D // TILES), Columns(ht.at[1], 0, D // TILES),
+                 Columns(ht.at[1], TILES // 2, D // TILES), *rest)
+        return layer_kernel(C, TILES, head, scale, 256, q_gain.shape[0], *r[:a], r[a:b], *r[b:c], r[c:d], *r[d:e], views, *r[e + 5:])
+
+    g_w, u_w, d_w, blk, ig, sums, q_w, kv_w, o_w = call(
+        layer, "layer", 1,
+        (S((2, C, R, D), BF), S((B, 2 * C * unit), BF), S((B, 2 * C * unit), BF), S((2 * C * unit, B), BF),
+         S((2, R, H), BF), S((2, R, H), BF), S((2,) + V, F32), S((B, 2 * C * head), BF), S((2, B, C * head), BF),
+         S((2 * C * head, B), BF)),
+        [VM] * 6 + [pl.BlockSpec(memory_space=pltpu.SMEM)] + [HBM] * 7, (HBM,) * 4 + (VM,) * 6,
+        [vm(16, B), vm(NB, 16, B), f32(R, H), f32(R, H), vm(2 * C, B, 2 * unit), vm(2 * C, unit, B)] + mine_s
+        + [vm(2, C * R, unit), vm(unit, D), vm(2, C, R, D), vm(2, C, R, D), vm(2, C, R, D), vm(D, 2 * unit),
+           f32(T, 128), f32(T, 128), f32(T, head)] + red(F32)
+        + [rs(), vm(R, H), vm(R, H), f32(6, R, 128), vm(2, C * R, 2 * unit), vm(2 * unit, T), vm(unit, T),
+           vm(C, 3 * unit, 2 * B)]
+        + [f32(8, T), wide(), wide(), wide(), one(), vm(2 * C, 2 * head, B), vm(2 * C, B, 2 * head), vm(2 * C, head, B),
+           vm(2 * C, head, B), f32(2, *V), f32(*V), f32(*V), f32(C, *V)]
+        + inner + [rs()],
+        layer_input, rows_of(attn_gain), rows_of(mlp_gain), small, cotangent, freq, block_pair,
+        q_weight, key_projection, value_projection, o_weight, gate_weight, up_weight, down_weight,
+    )[1:]
     few = q_gain.shape[0]
-    pick_few = lambda v: lax.dynamic_slice_in_dim(v, mine * few, few)
-    head_sums = sums[0, 2 * n_rows:] + sums[1, 2 * n_rows:]
-    return (
-        join(blk), join(ig).astype(F32), pick(both), q_w.astype(F32), kv_w[0].astype(F32), kv_w[1].astype(F32),
-        pick_few(head_sums[0]), pick_few(head_sums[1]), o_w.astype(F32), pick(both_mlp), g_w.astype(F32),
-        u_w.astype(F32), d_w.astype(F32),
-    )
+    wide_w = lambda v: S(v.shape, F32)
+    STEPS = 4
+    part = lambda *shape: pl.BlockSpec((shape[0] // STEPS,) + shape[1:], lambda i: (i,) + (0,) * (len(shape) - 1))
+    inner_part = lambda n, m, w: pl.BlockSpec((n, m // STEPS, w), lambda i: (0, i, 0))
+    same = lambda *shape: pl.BlockSpec(shape, lambda i: (0,) * len(shape))
+    kv_part = part(*kv_w.shape[1:])
+    out = pl.pallas_call(
+        functools.partial(finish_kernel, few), name="finish", grid=(STEPS,),
+        out_shape=(S((R, D), BF), S((R, D), F32), S((1, B), F32), wide_w(q_w), S(kv_w.shape[1:], F32),
+                   S(kv_w.shape[1:], F32), S((1, few), F32), S((1, few), F32), wide_w(o_w), S((1, B), F32),
+                   wide_w(g_w), wide_w(u_w), wide_w(d_w)),
+        in_specs=[inner_part(*blk.shape), inner_part(*ig.shape), same(*sums.shape), part(*g_w.shape), part(*u_w.shape),
+                  part(*d_w.shape), part(*q_w.shape), inner_part(*kv_w.shape), part(*o_w.shape)],
+        out_specs=(part(R, D), part(R, D), same(1, B), part(*q_w.shape), kv_part, kv_part, same(1, few), same(1, few),
+                   part(*o_w.shape), same(1, B), part(*g_w.shape), part(*u_w.shape), part(*d_w.shape)),
+        compiler_params=pltpu.CompilerParams(vmem_limit_bytes=60 * 1024 * 1024),
+    )(blk, ig, sums, g_w, u_w, d_w, q_w, kv_w, o_w)
+    return tuple(v.reshape(v.shape[1:]) if i in (2, 6, 7, 9) else v for i, v in enumerate(out))
 
 
 def fits(mesh_shape, layer_input, q_weight, key_projection, gate_weight):
@@ -1320,8 +1454,9 @@
     return (
         mesh_shape[FSDP] == 4 and mesh_shape[HEADS] == 2
         and key_projection.shape[1] == C * HEAD_SIZE and q_weight.shape[1] == 2 * C * HEAD_SIZE
-        and gate_weight.shape[1] % (2 * C * 128) == 0 and q_weight.shape[0] == 128
-        and layer_input.shape[0] % 128 == 0 and layer_input.shape[1] % (8 * 128) == 0
+        and gate_weight.shape[1] % (2 * C * 128) == 0 and 5 * gate_weight.shape[1] <= 2 * C * layer_input.shape[1]
+        and gate_weight.shape[1] >= 6 * C * 128 and q_weight.shape[0] == 128
+        and C == 4 and layer_input.shape[0] % 128 == 0 and layer_input.shape[1] % (8 * 128) == 0
     )
 
 

time: 425 us -> 363 us (0.85); the launches traced: 417 us -> 362 us
  Pallas kernels: 394 us -> 359 us
  other arithmetic: 15.5 us -> 1.27 us
  local copies, waits for them, and re-layouts: 6.22 us -> 1.25 us
    pallas_call x2 -> x1, Pallas kernels: 394 us -> 353 us  [call(): pl.pallas_call(kernel, name=name, out_shape=out_shape, in_specs=in_specs,...]
    convert_element_type x8 -> x1, other arithmetic: 7.46 us -> 1.27 us  [tensor_parallel(): jnp.pad(jnp.stack([q_gain, k_gain]), ((0, 6), (0, head - q_gain.shape[0])))]
    pallas_call x0 -> x1, Pallas kernels: none -> 5.7 us  [tensor_parallel(): pl.pallas_call(functools.partial(finish_kernel, few), name='finish', grid...]
where the time goes in v2:
time: 363 us; the launch traced here: 362 us
  Pallas kernels  359 us (99%)
    pallas_call x1, Pallas kernels, call(): pl.pallas_call(kernel, name=name, out_shape=out_shape, in_specs=in_specs,...  353 us

profile of v2, /device:TPU:0, one launch (start us, length us, event | category | flops | bytes accessed | tf_op | source)
XLA Modules:
  0.0 362.5 jit_solution(13497538381405666140)
XLA Ops:
  0.6 1.3 fusion.6.r_3_
  1.9 1.2 jit_solution_.3.r_5_
  3.2 353.4 %layer.1 = (bf16[2,4,128,2048]{3,2,1,0:T(8,128)(2,1)}, bf16[128,3072]{1,0:T(8,128)(2,1)}, bf16[128,3072]{1,0:T(8,128)(2,1)}, bf16[3072,128]{1,0:T(8,128)(2,1)}, ...) custom-call(bf16[128,2048]{1,0:T(8,128)(2,1)} %r_0_.1, ...), custom_call_target="tpu_custom_call" | custom-call | tf_op jit(solution)/shard_map/layer/pallas_call | solution.py:1356
  356.6 5.7 %finish.1 = (bf16[128,2048]{1,0:T(8,128)(2,1)}, f32[128,2048]{1,0:T(8,128)}, f32[1,128]{1,0:T(1,128)}, f32[128,1024]{1,0:T(8,128)}, f32[128,512]{1,0:T(8,128)}, ...) custom-call(bf16[2,128,1024]{2,1,0:T(8,128)(2,1)} %get-tuple-element, ...), custom_call_target="tpu_custom_call" | custom-call | tf_op jit(solution)/shard_map/finish/pallas_call | solution.py:1438

commit v3 on v2

--- a/solution.py
+++ b/solution.py
@@ -403,7 +403,7 @@
 MESH = pl.DeviceIdType.MESH
 HBM = pl.BlockSpec(memory_space=pltpu.HBM)
 VM = pl.BlockSpec(memory_space=pltpu.VMEM)
-SLOTS = 368
+SLOTS = 258
 LOCAL_SLOTS = 18
 NT = (((1,), (1,)), ((), ()))
 TN = (((0,), (0,)), ((), ()))
@@ -439,6 +439,11 @@
         self.used += count
         assert self.used <= SLOTS
         return self.used - count
+
+    def again(self, start, part):
+        top, self.used = self.used, start
+        next(part)
+        self.used = max(top, self.used)
 
     def slot(self):
         return self.slots(1)
@@ -857,6 +862,7 @@
             xg[kk, q, :, t] = (hat[:, b * B:(b + 1) * B] * gains[b].astype(F32)[0:1]).astype(BF)
 
     rows_x = gather_rows(net, x_ref, ht, False, normalise)
+    row_slots = net.used
     next(rows_x)
     h_qkv.post(2)
     for kk in range(2):
@@ -951,6 +957,7 @@
                        preferred_element_type=F32)
 
     reduce = reduce_rows(net, product, red, rs)
+    sum_slots = net.used
     next(reduce)
     h_mlp.relay(2)
     for _ in range(tiles // 2):
@@ -966,7 +973,7 @@
     h_out[...] = half
     hn[...] = times_gain(half * hs, gain_half(gains, y, 1, blocks // 2)).astype(BF)
     rows_h = gather_rows(net, hn, ht, True)
-    next(rows_h)
+    net.again(row_slots, rows_h)
     run(cots, rows_h)
     h_mlp.finish()
 
@@ -1042,7 +1049,7 @@
     keep.wait()
     hand_out = Deal(net, swiglu_groups(g_out, u_out, d_out, zgu, zd, unit))
     reduce = reduce_rows(net, normed, red, rs)
-    next(reduce)
+    net.again(sum_slots, reduce)
     for q in range(C):
         send_partial(q)
         steps_of(reduce, tiles // 2 // C)
@@ -1061,7 +1068,7 @@
     gh_out[...] = gh
     gb[...] = gh.astype(BF)
     rows_g = gather_rows(net, gb, xg, True)
-    next(rows_g)
+    net.again(row_slots, rows_g)
     add_partial(0)
     steps_of(rows_g, 2)
     add_partial(1)
@@ -1136,7 +1143,7 @@
         return jnp.dot(act[kk], wdd[:, lanes(t, w)], preferred_element_type=F32)
 
     reduce_d = reduce_rows(net, down, red, rs)
-    next(reduce_d)
+    net.again(sum_slots, reduce_d)
 
     def back_norm(grad, value, gain, r):
         rotated = grad * cosine[r] - pltpu.roll(grad, head // 2, 1) * sine[r]

time: 363 us -> 361 us (level)
  no operation moved by 1% of the time
where the time goes in v3:
time: 361 us; the launch traced here: 360 us
  Pallas kernels  357 us (99%)
    pallas_call x1, Pallas kernels, call(): pl.pallas_call(kernel, name=name, out_shape=out_shape, in_specs=in_specs,...  351 us

profile of v3, /device:TPU:0, one launch (start us, length us, event | category | flops | bytes accessed | tf_op | source)
XLA Modules:
  0.0 360.5 jit_solution(143956636138073586)
XLA Ops:
  0.6 1.3 fusion.6.r_3_
  1.9 1.2 jit_solution_.3.r_5_
  3.2 351.4 %layer.1 = (bf16[2,4,128,2048]{3,2,1,0:T(8,128)(2,1)}, bf16[128,3072]{1,0:T(8,128)(2,1)}, bf16[128,3072]{1,0:T(8,128)(2,1)}, bf16[3072,128]{1,0:T(8,128)(2,1)}, ...) custom-call(bf16[128,2048]{1,0:T(8,128)(2,1)} %r_0_.1, ...), custom_call_target="tpu_custom_call" | custom-call | tf_op jit(solution)/shard_map/layer/pallas_call | solution.py:1363
  354.6 5.7 %finish.1 = (bf16[128,2048]{1,0:T(8,128)(2,1)}, f32[128,2048]{1,0:T(8,128)}, f32[1,128]{1,0:T(1,128)}, f32[128,1024]{1,0:T(8,128)}, f32[128,512]{1,0:T(8,128)}, ...) custom-call(bf16[2,128,1024]{2,1,0:T(8,128)(2,1)} %get-tuple-element, ...), custom_call_target="tpu_custom_call" | custom-call | tf_op jit(solution)/shard_map/finish/pallas_call | solution.py:1445
